TPU v7x, 256 devices: a whole 4x4x8 slice. The times are simulated.
256 devices in a mesh: lat: 32 (over y, x, core), lev: 8 (over z).
Axes of the slice: x: 4, y: 4, z: 8, core: 2. Of those that a mesh axis runs over, the one named last changes fastest.
Arguments:
- fields: float32 [12, 128, 256, 1024], P(None, 'lev', 'lat'), may hold values from -6 to 6
- legendre: bfloat16 [256, 256, 256], P('lat'), as said below
- owner_counts: int32 [32], replicated, may hold values from 1 to 16, 256 in all
Outputs:
- covariance: float32 [512, 128, 128], P('lat', 'lev')
Inputs may be any that keep to these rules, and one draw needn't show every extreme that they name: `owner_counts`: each owner holds 1 to 16 total wavenumbers, the counts sum to 256, and some owner holds exactly 16. legendre[lat, m, n] is zero where n < m.
All inputs are finite; a program needn't handle non-finite values.
Results may differ from a plain program's by a relative error of at most 0.0038.
Values may be sent and summed in bfloat16 or wider, within the bound.
No kernel may reach another device: no remote copies, remote signals or barrier semaphores. Data moves between devices by JAX's collectives and lax.ppermute only.
A program may use at most 128 MiB of HBM per device.

v0:
```python
import math

import jax
import jax.numpy as jnp
from jax import lax
from jax.sharding import PartitionSpec as P


def in_blocks(x, dim, length):
    before, after = (x.shape[:dim], x.shape[dim + 1 :])
    return jnp.moveaxis(x.reshape(*before, length, -1, *after), dim, 0)


def summed_on_arrival(x, axis, dim):
    parts = in_blocks(x, dim, lax.axis_size(axis))
    arrived = lax.all_to_all(parts, axis, split_axis=0, concat_axis=0, tiled=True)
    return arrived.astype(jnp.float32).sum(axis=0)


def fourier_table(points, modes):
    places = jnp.arange(points, dtype=jnp.int32)
    orders = jnp.arange(modes, dtype=jnp.int32)
    phase = places[:, None] * orders[None, :] % points
    angle = phase.astype(jnp.float32) * (2.0 * math.pi / points)
    factor = points ** (-0.5)
    return jnp.stack([jnp.cos(angle) * factor, -jnp.sin(angle) * factor], axis=2)


def on_device(fields, legendre, owner_counts):
    members, lev_rows, lat_rows, points = fields.shape
    modes = legendre.shape[1]
    lev_count = lax.axis_size("lev")
    owners = owner_counts.shape[0]
    capacity = 2 * modes // owners
    dft_table = fourier_table(points, modes)
    spectra = jnp.einsum("belx,xmc->lmcbe", fields, dft_table, precision=lax.Precision.HIGHEST)
    spectra = spectra.reshape(lat_rows, modes, 2 * members * lev_rows).astype(jnp.bfloat16)
    collected_rows, transform_table_rows = (
        lax.all_to_all(spectra, "lat", split_axis=1, concat_axis=0, tiled=True),
        lax.all_to_all(legendre, "lat", split_axis=1, concat_axis=0, tiled=True),
    )
    wavenumber_rows = jnp.einsum(
        "dez,det->tez", collected_rows, transform_table_rows, preferred_element_type=jnp.float32
    )
    resident_modes = wavenumber_rows.shape[1]
    shaped = wavenumber_rows.reshape(modes, resident_modes, 2, members, lev_rows)
    anomaly = (shaped - jnp.mean(shaped, axis=3, keepdims=True)).astype(jnp.bfloat16)
    anomaly = anomaly.reshape(modes, resident_modes, 2 * members * lev_rows)
    starts = jnp.cumsum(owner_counts) - owner_counts
    offset = jnp.arange(capacity, dtype=jnp.int32)
    active_flag = offset[None, :] < owner_counts[:, None]
    slot_index = jnp.where(active_flag, starts[:, None] + offset[None, :], 0).reshape(-1)
    slotted = jnp.take(anomaly, slot_index, axis=0)
    slotted = jnp.where(active_flag.reshape(-1)[:, None, None], slotted, jnp.zeros_like(slotted))
    slotted = slotted[None]
    received = lax.all_to_all(
        lax.all_to_all(slotted, "lat", split_axis=1, concat_axis=2, tiled=True),
        "lev",
        split_axis=2,
        concat_axis=0,
        tiled=True,
    )
    mode_share = received.shape[2]
    blocks = received.reshape(lev_count, capacity, mode_share, 2 * members, lev_rows)
    partial_value = jnp.einsum(
        "esaql,fsaqk->selfk", blocks, blocks, preferred_element_type=jnp.float32
    )
    partial_value = partial_value.reshape(capacity, lev_count * lev_rows, lev_count * lev_rows)
    summed = summed_on_arrival(partial_value.astype(jnp.bfloat16), "lev", 1)
    owner = lax.axis_index("lat")
    wavenumber = starts[owner] + offset
    live_count = owner_counts[owner]
    divisor = ((members - 1) * (2 * wavenumber + 2)).astype(jnp.float32)
    scaled = summed / divisor[:, None, None]
    return jnp.where((offset < live_count)[:, None, None], scaled, jnp.zeros_like(scaled))


def solution(mesh):
    return jax.shard_map(
        on_device,
        mesh=mesh,
        in_specs=(P(None, "lev", "lat", None), P("lat", None, None), P()),
        out_specs=P("lat", "lev", None),
        check_vma=False,
    )
```

profile of v0, /device:TPU:1, one launch (start us, length us, event | category | flops | bytes accessed | tf_op | source)
XLA Modules:
  0.0 276.8 jit_solution(14894597749513370844)
XLA Ops:
  0.0 4.2 %negate_multiply_fusion = (f32[1024,256,1]{1,0,2:T(8,128)S(1)}, f32[1024,256,1]{1,0,2:T(8,128)S(1)}) fusion(), kind=kLoop, calls=%fused_computation.27 | loop fusion | flops 4456448 | bytes 2097152 | tf_op jit(solution)/shard_map/mul | solution.py:26
  4.2 15.6 %fusion.13 = bf16[8,256,2,12,16]{1,4,0,3,2:T(8,128)(2,1)S(1)} fusion(f32[12,16,8,1024]{3,2,1,0:T(8,128)} %param.3, f32[1024,256,1]{1,0,2:T(8,128)S(1)} %get-tuple-element.7, f32[1024,256,1]{1,0,2:T(8,128)S(1)} %get-tuple-element.8), kind=kOutput, calls=%fused_computation.20 | convolution fusion | flops 9664987136 | bytes 9961472 | tf_op jit(solution)/shard_map/belx,xmc->lmcbe/dot_general | solution.py:36
  19.8 0.2 copy.20
  20.0 0.0 copy-start.1
  20.0 2.1 copy.21
  22.1 0.0 copy-start.2
  22.1 8.7 %all-to-all-start = ((bf16[8,256,384]{2,0,1:T(8,128)(2,1)}), bf16[8,256,384]{2,0,1:T(8,128)(2,1)S(1)}, u32[]{:S(2)}, u32[]{:S(2)}) async-start(bf16[8,256,384]{2,0,1:T(8,128)(2,1)} %copy.21), calls=%async_computation | async-start | bytes 3145728 | tf_op jit(solution)/shard_map/all_to_all | solution.py:39
  30.8 0.0 copy-done.1
  30.8 1.5 copy.24
  32.3 20.6 %all-to-all-done = bf16[8,256,384]{2,0,1:T(8,128)(2,1)S(1)} async-done(((bf16[8,256,384]{2,0,1:T(8,128)(2,1)}), bf16[8,256,384]{2,0,1:T(8,128)(2,1)S(1)}, u32[]{:S(2)}, u32[]{:S(2)}) %all-to-all-start) | async-done | bytes 1572896 | tf_op jit(solution)/shard_map/all_to_all | solution.py:39
  53.0 5.5 %all-to-all-start.1 = ((bf16[8,256,256]{2,0,1:T(8,128)(2,1)}), bf16[8,256,256]{2,0,1:T(8,128)(2,1)S(1)}, u32[]{:S(2)}, u32[]{:S(2)}) async-start(bf16[8,256,256]{2,0,1:T(8,128)(2,1)} %copy.24), calls=%async_computation.1 | async-start | bytes 2097152 | tf_op jit(solution)/shard_map/all_to_all | solution.py:40
  58.5 0.0 copy-done.2
  58.5 0.1 copy.18
  58.6 0.1 reduce-window.9
  58.7 0.1 reduce
  58.8 0.1 iota_add_fusion
  58.9 0.1 select_n.90
  59.0 0.1 add.89
  59.0 0.1 iota_compare_fusion
  59.1 0.1 lt.78
  59.3 1.4 copy.23
  60.7 15.0 %all-to-all-done.1 = bf16[8,256,256]{2,0,1:T(8,128)(2,1)S(1)} async-done(((bf16[8,256,256]{2,0,1:T(8,128)(2,1)}), bf16[8,256,256]{2,0,1:T(8,128)(2,1)S(1)}, u32[]{:S(2)}, u32[]{:S(2)}) %all-to-all-start.1) | async-done | bytes 1048608 | tf_op jit(solution)/shard_map/all_to_all | solution.py:40
  75.7 0.0 copy-start
  75.7 1.0 copy-done
  76.6 2.4 fusion.11
  79.1 0.4 reduce_sum.18
  79.5 1.5 fusion.5
  81.0 2.2 copy.27
  83.2 3.2 %gather_fusion = bf16[512,8,384]{2,1,0:T(8,128)(2,1)} fusion(bf16[256,8,384]{2,1,0:T(8,128)(2,1)S(1)} %copy.27, s32[1024]{0:T(1024)S(1)} %pad_clamp_fusion), kind=kCustom, calls=%fused_computation | custom fusion | bytes 6293504 | tf_op jit(solution)/shard_map/jit(_take)/gather | solution.py:53
  86.3 4.8 %fusion.4 = bf16[1,512,8,384]{3,2,0,1:T(8,128)(2,1)S(1)} fusion(bf16[512,8,384]{2,1,0:T(8,128)(2,1)} %gather_fusion, pred[512]{0:T(512)(128)(4,1)S(1)} %compare_and_fusion, pred[512]{0:T(512)(128)(4,1)S(1)} %lt.78), kind=kLoop, calls=%fused_computation.7 | loop fusion | flops 3145728 | bytes 6292480 | tf_op jit(solution)/shard_map/jit(_where)/select_n | solution.py:54
  91.1 43.1 %all_to_all.74 = bf16[1,512,8,384]{3,2,0,1:T(8,128)(2,1)S(1)} all-to-all(bf16[1,512,8,384]{3,2,0,1:T(8,128)(2,1)S(1)} %fusion.4), channel_id=1, replica_groups=mesh['lat'=32,'lev'=8] {'lat'}, dimensions={1} | all-to-all | bytes 6291456 | tf_op jit(solution)/shard_map/all_to_all | solution.py:57
  134.2 0.5 copy.55
  134.7 1.9 copy.30
  136.6 80.8 %all_to_all.75 = bf16[1,16,256,384]{3,1,0,2:T(8,128)(2,1)S(1)} all-to-all(bf16[1,16,256,384]{3,1,0,2:T(8,128)(2,1)S(1)} %copy.30), channel_id=1, replica_groups=mesh['lat'=32,'lev'=8] {'lev'}, dimensions={2} | all-to-all | bytes 6291456 | tf_op jit(solution)/shard_map/all_to_all | solution.py:56
  217.4 0.7 copy.31
  218.1 8.6 %copy.32 = bf16[8,1,16,32,384]{3,4,0,2,1:T(8,128)(2,1)} copy(bf16[8,1,16,32,384]{4,3,0,2,1:T(8,128)(2,1)S(1)} %bitcast.78) | data formatting | bytes 6291456 | tf_op jit(solution)/shard_map/all_to_all | solution.py:56
  226.7 19.8 %bitcast_convert_fusion = bf16[16,8,16,8,16]{4,2,3,1,0:T(8,128)(2,1)S(1)} fusion(bf16[8,16,32,24,16,1]{2,4,3,5,0,1:T(8,128)(2,1)} %bitcast.76, bf16[8,16,32,24,16,1]{2,4,3,0,5,1:T(8,128)(2,1)} %bitcast.77), kind=kOutput, calls=%fused_computation.1 | convolution fusion | flops 402915328 | bytes 6815744 | tf_op jit(solution)/shard_map/esaql,fsaqk->selfk/dot_general | solution.py:65
  246.6 4.0 %copy.33 = bf16[16,8,16,8,16]{4,3,2,1,0:T(8,128)(2,1)} copy(bf16[16,8,16,8,16]{4,2,3,1,0:T(8,128)(2,1)S(1)} %bitcast_convert_fusion) | data formatting | bytes 1048576 | tf_op jit(solution)/shard_map/convert_element_type | solution.py:69
  250.6 5.1 %convert_element_type.52 = bf16[16,8,16,128]{3,2,1,0:T(8,128)(2,1)S(1)} reshape(bf16[16,8,16,8,16]{4,3,2,1,0:T(8,128)(2,1)} %copy.33) | data formatting | bytes 1048576 | tf_op jit(solution)/shard_map/convert_element_type | solution.py:69
  255.7 0.8 copy.34
  256.5 3.5 %all-to-all-start.4 = ((bf16[8,16,16,128]{3,2,1,0:T(8,128)(2,1)}), bf16[8,16,16,128]{3,2,1,0:T(8,128)(2,1)S(1)}, u32[]{:S(2)}, u32[]{:S(2)}) async-start(bf16[8,16,16,128]{3,2,1,0:T(8,128)(2,1)} %copy.34), calls=%async_computation.4 | async-start | bytes 1048576 | tf_op jit(solution)/shard_map/all_to_all | solution.py:16
  260.0 0.6 dynamic_slice.7
  260.6 0.7 dynamic_slice.6
  261.3 0.7 multiply_convert_fusion
  262.0 0.7 iota_compare_fusion.1
  262.7 13.3 %all-to-all-done.4 = bf16[8,16,16,128]{3,2,1,0:T(8,128)(2,1)S(1)} async-done(((bf16[8,16,16,128]{3,2,1,0:T(8,128)(2,1)}), bf16[8,16,16,128]{3,2,1,0:T(8,128)(2,1)S(1)}, u32[]{:S(2)}, u32[]{:S(2)}) %all-to-all-start.4) | async-done | bytes 524320 | tf_op jit(solution)/shard_map/all_to_all | solution.py:16
  276.0 0.1 convert_reduce_fusion
  276.0 0.8 divide_select_fusion
  (5 shorter events, 0.1 us)
Async XLA Ops:
  20.0 10.8 %copy-start.1 = (bf16[8,256,256]{2,1,0:T(8,128)(2,1)S(1)}, bf16[8,256,256]{2,1,0:T(8,128)(2,1)}, u32[]{:S(2)}) copy-start(bf16[8,256,256]{2,1,0:T(8,128)(2,1)} %param.4) | copy-start | bytes 3145732
  22.1 36.5 %copy-start.2 = (s32[32]{0:T(128)S(1)}, s32[32]{0:T(128)}, u32[]{:S(2)}) copy-start(s32[32]{0:T(128)} %param.5) | copy-start | bytes 388
  22.1 30.9 %all-to-all-start = ((bf16[8,256,384]{2,0,1:T(8,128)(2,1)}), bf16[8,256,384]{2,0,1:T(8,128)(2,1)S(1)}, u32[]{:S(2)}, u32[]{:S(2)}) async-start(bf16[8,256,384]{2,0,1:T(8,128)(2,1)} %copy.21), calls=%async_computation | async-start | bytes 3145728 | tf_op jit(solution)/shard_map/all_to_all | solution.py:39
  53.0 22.7 %all-to-all-start.1 = ((bf16[8,256,256]{2,0,1:T(8,128)(2,1)}), bf16[8,256,256]{2,0,1:T(8,128)(2,1)S(1)}, u32[]{:S(2)}, u32[]{:S(2)}) async-start(bf16[8,256,256]{2,0,1:T(8,128)(2,1)} %copy.24), calls=%async_computation.1 | async-start | bytes 2097152 | tf_op jit(solution)/shard_map/all_to_all | solution.py:40
  75.7 1.0 copy-start
  256.5 19.4 %all-to-all-start.4 = ((bf16[8,16,16,128]{3,2,1,0:T(8,128)(2,1)}), bf16[8,16,16,128]{3,2,1,0:T(8,128)(2,1)S(1)}, u32[]{:S(2)}, u32[]{:S(2)}) async-start(bf16[8,16,16,128]{3,2,1,0:T(8,128)(2,1)} %copy.34), calls=%async_computation.4 | async-start | bytes 1048576 | tf_op jit(solution)/shard_map/all_to_all | solution.py:16
where the time goes:
time: 279 us; the launch traced here: 277 us
  blocking collectives  124 us (44%)
  waiting for transfers between devices  48.9 us (18%)
  matrix products  37.9 us (14%)
  local copies, waits for them, and re-layouts  34.8 us (12%)
  starting transfers between devices  17.7 us (6%)
  other arithmetic  13.4 us (5%)
    all_to_all x1, blocking collectives, on_device(): lax.all_to_all(lax.all_to_all(slotted, 'lat', split_axis=1, concat_axis=2...  80.8 us
    all_to_all x1, blocking collectives, on_device(): lax.all_to_all(slotted, 'lat', split_axis=1, concat_axis=2, tiled=True)  43.1 us
    all_to_all x1, waiting for transfers between devices, on_device(): lax.all_to_all(spectra, 'lat', split_axis=1, concat_axis=0, tiled=True)  20.6 us
    dot_general x1, matrix products, on_device(): jnp.einsum('esaql,fsaqk->selfk', blocks, blocks, preferred_element_type=j...  19.8 us
    dot_general x1, matrix products, on_device(): jnp.einsum('belx,xmc->lmcbe', fields, dft_table, precision=lax.Precision....  15.6 us
    all_to_all x1, waiting for transfers between devices, on_device(): lax.all_to_all(legendre, 'lat', split_axis=1, concat_axis=0, tiled=True)  15 us
    all_to_all x1, waiting for transfers between devices, summed_on_arrival(): lax.all_to_all(parts, axis, split_axis=0, concat_axis=0, tiled=True)  13.3 us
    all_to_all x2, local copies, waits for them, and re-layouts, on_device(): lax.all_to_all(lax.all_to_all(slotted, 'lat', split_axis=1, concat_axis=2...  9.36 us
  transfers between devices with their start and end apart: 3, of which 3 were waited for; matrix products, arithmetic and copies ran while one was open for 2% of the time, Pallas kernels for 0%

commit v1 on v0

v1 whole, which is shorter than its diff:
```python
import functools
import math

import jax
import jax.numpy as jnp
import ml_dtypes
import numpy as np
from jax import lax
from jax.experimental import pallas as pl
from jax.experimental.pallas import tpu as pltpu
from jax.sharding import PartitionSpec as P

F32, BF16 = jnp.float32, jnp.bfloat16
LATS, LEVS = 32, 8
STRIDE = 32
BLOCKS = 8
SPEC_ROWS, LEG_ROWS = 64, 24
ROWS = SPEC_ROWS + LEG_ROWS
SLOT_ROWS, USED_ROWS = 16, 14
VMEM = pltpu.VMEM


def fourier_tables(points, modes):
    half = points // 2
    j = np.arange(half)
    tables = []
    for parity in range(2):
        d = 2 * np.arange(LATS // 2) + parity
        m = (d[:, None] + STRIDE * np.arange(BLOCKS)[None, :]).reshape(-1)
        angle = (m[:, None] * j[None, :] % points) * (2.0 * math.pi / points)
        tables.append(np.concatenate([np.cos(angle), -np.sin(angle)]) * points**-0.5)
    table = np.stack(tables)
    high = table.astype(np.float32).astype(ml_dtypes.bfloat16)
    low = (table - high.astype(np.float64)).astype(np.float32).astype(ml_dtypes.bfloat16)
    return high, low


def dot_nt(a, b):
    return lax.dot_general(a, b, (((1,), (1,)), ((), ())), preferred_element_type=F32)


def dot_tn(a, b):
    return lax.dot_general(a, b, (((0,), (0,)), ((), ())), preferred_element_type=F32)


def dot_nn(a, b):
    return lax.dot_general(a, b, (((1,), (0,)), ((), ())), preferred_element_type=F32)


def fourier_kernel(members, lev_rows, lat_rows, pieces, *refs):
    f_refs, (leg_ref, hi_ref, lo_ref, out_ref, uhi, ulo, t_ref) = refs[:pieces], refs[pieces:]
    b = pl.program_id(0)
    rows = pl.ds(pl.multiple_of(b * lev_rows, lev_rows), lev_rows)
    for piece in range(pieces // 2):
        lanes = slice(piece * 128, (piece + 1) * 128)
        for lat in range(lat_rows):
            every = pl.ds(lat, lev_rows, stride=lat_rows)
            left, right = f_refs[piece][0, every, :], f_refs[piece + pieces // 2][0, every, :]
            for parity, u in enumerate((left + right, left - right)):
                high = u.astype(BF16)
                uhi[parity, lat, rows, lanes] = high
                ulo[parity, lat, rows, lanes] = (u - high.astype(F32)).astype(BF16)

    @pl.when(b < lat_rows)
    def _():
        table = leg_ref[0].astype(F32)
        lane = lax.broadcasted_iota(jnp.int32, (STRIDE, 2 * 128), 1)

        def block(i):
            return table[STRIDE * i : STRIDE * (i + 1), :]

        tiles = [block(0)[:, :128], block(0)[:, 128:]]
        for p in range(1, BLOCKS // 2):
            other = pltpu.roll(block(BLOCKS - p), STRIDE * p, 1)
            packed = jnp.where(lane >= STRIDE * p, block(p), other)
            tiles += [packed[:, :128], packed[:, 128:]]
        tiles.append(block(BLOCKS // 2)[:, 128:])
        for t, tile in enumerate(tiles):
            first = SPEC_ROWS + (t // 3) * lat_rows
            t_ref[t % 3, pl.ds(first + b, LATS, stride=ROWS), :] = tile

    @pl.when(b == members - 1)
    def _():
        count = LATS // 2 * BLOCKS
        for lat in range(lat_rows):
            for parity in range(2):
                h, l = uhi[parity, lat], ulo[parity, lat]
                acc = dot_nt(hi_ref[parity], h) + (dot_nt(hi_ref[parity], l) + dot_nt(lo_ref[parity], h))
                both = jnp.concatenate([acc[:count], acc[count:]], axis=1)
                for pair in range(LATS // 2):
                    start = (2 * pair + parity) * ROWS + lat
                    for t in range(3):
                        t_ref[t, pl.ds(start, BLOCKS, stride=lat_rows), :] = both[
                            pair * BLOCKS : (pair + 1) * BLOCKS, t * 128 : (t + 1) * 128
                        ]
        for t in range(3):
            for d in range(LATS):
                rows = slice(d * ROWS, (d + 1) * ROWS)
                out_ref[rows, t * 128 : (t + 1) * 128] = t_ref[t, rows, :].astype(BF16)


def fourier(fields, legendre):
    members, lev_rows, lat_rows, points = fields.shape
    modes = legendre.shape[1]
    columns, pieces = 2 * members * lev_rows, points // 128
    rows = fields.reshape(members, lev_rows * lat_rows, points)
    high, low = fourier_tables(points, modes)
    whole = lambda *shape: pl.BlockSpec(shape, lambda b: (0,) * len(shape))
    return pl.pallas_call(
        functools.partial(fourier_kernel, members, lev_rows, lat_rows, pieces),
        grid=(members,),
        in_specs=[
            pl.BlockSpec((1, lev_rows * lat_rows, 128), lambda b, piece=piece: (b, 0, piece))
            for piece in range(pieces)
        ]
        + [
            pl.BlockSpec((1, modes, modes), lambda b: (jnp.minimum(b, lat_rows - 1), 0, 0)),
            whole(*high.shape),
            whole(*low.shape),
        ],
        out_specs=whole(LATS * ROWS, columns),
        out_shape=jax.ShapeDtypeStruct((LATS * ROWS, columns), BF16),
        scratch_shapes=[
            VMEM((2, lat_rows, members * lev_rows, points // 2), BF16),
            VMEM((2, lat_rows, members * lev_rows, points // 2), BF16),
            VMEM((3, LATS * ROWS, 128), F32),
        ],
        compiler_params=pltpu.CompilerParams(vmem_limit_bytes=40 << 20),
        cost_estimate=pl.CostEstimate(flops=5 * 10**9, bytes_accessed=10**7, transcendentals=0),
        name="fourier",
    )(*[rows] * pieces, legendre, jnp.asarray(high), jnp.asarray(low))


def place(i, j):
    p = min(j, BLOCKS - 1 - j)
    base = 3 * i if j < BLOCKS // 2 else 3 * (p + 1) + 3 * i
    return [(2 * p + (base + t) // USED_ROWS, (base + t) % USED_ROWS) for t in range(3)]


def legendre_kernel(members, lev_rows, lat_rows, r_ref, out_ref, t_ref):
    columns = r_ref.shape[2]
    lats = LATS * lat_rows

    def rows_of(first, lanes):
        x = r_ref[:, first : first + lat_rows, lanes].astype(F32)
        return x.reshape(lats, -1).astype(BF16)

    def table(t):
        return rows_of(SPEC_ROWS + (t // 3) * lat_rows, slice((t % 3) * 128, (t % 3 + 1) * 128))

    def spectra(i):
        return rows_of(i * lat_rows, slice(0, columns))

    row = lax.broadcasted_iota(jnp.int32, (columns, columns), 0)
    col = lax.broadcasted_iota(jnp.int32, (columns, columns), 1)
    half = members * lev_rows
    same = ((row >= half) == (col >= half)) & (row % lev_rows == col % lev_rows)
    ones = jnp.where(same, 1.0, 0.0).astype(BF16)

    zero = jnp.zeros((LATS, 128), F32)
    for k in range(2 * BLOCKS // 2):
        for r in range(USED_ROWS - (k % 2), SLOT_ROWS):
            t_ref[pl.ds(k * SLOT_ROWS + r, LATS, stride=LEVS * SLOT_ROWS), :] = zero

    def finish(waves, units):
        high = waves.astype(BF16)
        low = (waves - high.astype(F32)).astype(BF16)
        total = dot_nn(high, ones) + dot_nn(low, ones)
        anomaly = waves - total * (1.0 / members)
        for u, (i, j) in enumerate(units):
            for t, (k, r) in enumerate(place(i, j)):
                t_ref[pl.ds(k * SLOT_ROWS + r, LATS, stride=LEVS * SLOT_ROWS), :] = anomaly[
                    u * STRIDE : (u + 1) * STRIDE, t * 128 : (t + 1) * 128
                ]

    for p in range(BLOCKS // 2):
        first, second = table(2 * p), table(2 * p + 1)
        mine = spectra(p)
        lower, upper = dot_tn(first, mine), dot_tn(second, mine)
        units = [(p, j) for j in range(p, BLOCKS)]
        if p:
            other = dot_tn(first, spectra(BLOCKS - p))
            lower = jnp.concatenate([other[: STRIDE * p], lower[STRIDE * p :]], axis=0)
            units = [(BLOCKS - p, BLOCKS - p + g) for g in range(p)] + units
        finish(lower, units[:4])
        finish(upper, units[4:])
    p = BLOCKS // 2
    finish(dot_tn(table(2 * p), spectra(p)), [(p, j) for j in range(p, BLOCKS)])
    step = LEVS * SLOT_ROWS
    for c in range(LATS):
        out_ref[c * step : (c + 1) * step, :] = t_ref[c * step : (c + 1) * step, :].astype(BF16)


def legendre_stage(received, members, lev_rows, lat_rows):
    rows = LATS * LEVS * SLOT_ROWS
    return pl.pallas_call(
        functools.partial(legendre_kernel, members, lev_rows, lat_rows),
        in_specs=[pl.BlockSpec(memory_space=VMEM)],
        out_specs=pl.BlockSpec(memory_space=VMEM),
        out_shape=jax.ShapeDtypeStruct((rows, 128), BF16),
        scratch_shapes=[VMEM((rows, 128), F32)],
        compiler_params=pltpu.CompilerParams(vmem_limit_bytes=40 << 20),
        cost_estimate=pl.CostEstimate(flops=2 * 10**9, bytes_accessed=4 * 10**6, transcendentals=0),
        name="legendre",
    )(received)


def home(lev):
    p, h = lev // 2, lev % 2
    return p, h


def covariance_kernel(members, lev_rows, y_ref, out_ref):
    levels = LEVS * lev_rows
    count = LATS * SLOT_ROWS
    lev, lat = lax.axis_index("lev"), lax.axis_index("lat")
    p, h = home(lev)
    parts = [y_ref[:, v].reshape(count, 128) for v in range(LEVS)]
    lane = lax.broadcasted_iota(jnp.int32, (count, 128), 1)
    for bit in (1, 2, 4):
        shift = bit * lev_rows
        low = (lane // shift) % 2 == 0
        swapped = list(parts)
        for v in range(LEVS):
            if v & bit:
                continue
            a, b = parts[v], parts[v | bit]
            swapped[v] = jnp.where(low, a, pltpu.roll(b, shift, 1))
            swapped[v | bit] = jnp.where(low, pltpu.roll(a, 128 - shift, 1), b)
        parts = swapped
    first_rows = jnp.where(h == 0, 3 * (p + 1), 0)
    slot = lax.broadcasted_iota(jnp.int32, (levels, count), 1) % SLOT_ROWS
    is_first = slot < first_rows
    one = jnp.zeros((levels, levels), F32)
    two = jnp.zeros((levels, levels), F32)
    for part in parts:
        part = part.astype(BF16)
        turned = part.astype(F32).T
        zero = jnp.zeros_like(turned)
        one += dot_nn(jnp.where(is_first, turned, zero).astype(BF16), part)
        two += dot_nn(jnp.where(is_first, zero, turned).astype(BF16), part)
    for s, (total, n) in enumerate(((one, lat + STRIDE * p), (two, lat + STRIDE * (BLOCKS - 1 - p)))):
        divisor = ((members - 1) * (2 * n + 2)).astype(F32)
        scaled = total / jnp.full((levels, levels), divisor, F32)
        for v in range(LEVS):
            out_ref[v, s * lev_rows : (s + 1) * lev_rows, :] = scaled[v * lev_rows : (v + 1) * lev_rows]


def covariance_stage(received, members, lev_rows):
    return pl.pallas_call(
        functools.partial(covariance_kernel, members, lev_rows),
        in_specs=[pl.BlockSpec(memory_space=VMEM)],
        out_specs=pl.BlockSpec(memory_space=VMEM),
        out_shape=jax.ShapeDtypeStruct((LEVS, 2 * lev_rows, 128), F32),
        compiler_params=pltpu.CompilerParams(vmem_limit_bytes=40 << 20),
        cost_estimate=pl.CostEstimate(flops=10**9, bytes_accessed=2 * 10**6, transcendentals=0),
        name="covariance",
    )(received)


def route_kernel(lev_rows, counts_ref, g_ref, out_ref, f_ref):
    lat = lax.axis_index("lat")
    half = BLOCKS // 2
    for j in range(BLOCKS):
        p, s = min(j, BLOCKS - 1 - j), int(j >= half)
        rows = slice(s * lev_rows, (s + 1) * lev_rows)
        f_ref[j] = g_ref[2 * p, rows, :] + g_ref[2 * p + 1, rows, :]

    def step(owner, start):
        j = jnp.maximum(start - lat + (STRIDE - 1), 0) // STRIDE
        out_ref[owner] = f_ref[jnp.minimum(j, BLOCKS - 1)]
        return start + counts_ref[owner]

    lax.fori_loop(0, LATS, step, jnp.int32(0))


def route_stage(parts, owner_counts, lev_rows):
    return pl.pallas_call(
        functools.partial(route_kernel, lev_rows),
        in_specs=[pl.BlockSpec(memory_space=pltpu.SMEM), pl.BlockSpec(memory_space=VMEM)],
        out_specs=pl.BlockSpec(memory_space=VMEM),
        out_shape=jax.ShapeDtypeStruct((LATS, lev_rows, 128), F32),
        scratch_shapes=[VMEM((BLOCKS, lev_rows, 128), F32)],
        name="route",
    )(owner_counts, parts)


def collect_kernel(counts_ref, r_ref, out_ref):
    lat = lax.axis_index("lat")
    start = lax.fori_loop(0, lat, lambda k, s: s + counts_ref[k], jnp.int32(0))
    count = counts_ref[lat]
    for slot in range(out_ref.shape[0]):
        block = r_ref[(start + slot) % STRIDE]
        out_ref[slot] = jnp.where(slot < count, block, jnp.zeros_like(block))


def collect_stage(routed, owner_counts, capacity, lev_rows):
    return pl.pallas_call(
        collect_kernel,
        in_specs=[pl.BlockSpec(memory_space=pltpu.SMEM), pl.BlockSpec(memory_space=VMEM)],
        out_specs=pl.BlockSpec(memory_space=VMEM),
        out_shape=jax.ShapeDtypeStruct((capacity, lev_rows, 128), F32),
        name="collect",
    )(owner_counts, routed)


def exchange(x, axis):
    return lax.all_to_all(x, axis, split_axis=0, concat_axis=0, tiled=True)


def on_device(fields, legendre, owner_counts):
    members, lev_rows, lat_rows, _ = fields.shape
    modes = legendre.shape[1]
    capacity = 2 * modes // owner_counts.shape[0]
    first = fourier(fields, legendre)
    first = exchange(first.reshape(LATS, ROWS, -1), "lat")
    second = legendre_stage(first, members, lev_rows, lat_rows)
    second = exchange(second.reshape(LATS * LEVS, SLOT_ROWS, 128), ("lat", "lev"))
    third = covariance_stage(second.reshape(LATS, LEVS, SLOT_ROWS, 128), members, lev_rows)
    third = exchange(third, "lev")
    fourth = route_stage(third, owner_counts, lev_rows)
    fourth = exchange(fourth, "lat")
    return collect_stage(fourth, owner_counts, capacity, lev_rows)


def solution(mesh):
    return jax.shard_map(
        on_device,
        mesh=mesh,
        in_specs=(P(None, "lev", "lat", None), P("lat", None, None), P()),
        out_specs=P("lat", "lev", None),
        check_vma=False,
    )
```

time: 279 us -> 130 us (0.47)
  waiting for transfers between devices: 48.9 us -> 0 us
  matrix products: 37.9 us -> 0 us
  local copies, waits for them, and re-layouts: 34.8 us -> 6.09 us
  starting transfers between devices: 17.7 us -> 0 us
  blocking collectives: 124 us -> 107 us
  Pallas kernels: 0 us -> 16.5 us
  other arithmetic: 13.4 us -> 0 us
    all_to_all x3 -> x0, waiting for transfers between devices: 48.9 us -> none  [the longest x1 20.6 us: on_device(): lax.all_to_all(spectra, 'lat', split_axis=1, concat_axis=0, tiled=True)]
    dot_general x3 -> x0, matrix products: 37.9 us -> none  [the longest x1 19.8 us: on_device(): jnp.einsum('esaql,fsaqk->selfk', blocks, blocks, preferred_element_type=j...]
    all_to_all x3 -> x0, starting transfers between devices: 17.7 us -> none  [the longest x1 8.71 us: on_device(): lax.all_to_all(spectra, 'lat', split_axis=1, concat_axis=0, tiled=True)]
    all_to_all x2 -> x4, blocking collectives: 124 us -> 107 us  [exchange(): return lax.all_to_all(x, axis, split_axis=0, concat_axis=0, tiled=True)]
    pallas_call x0 -> x5, Pallas kernels: none -> 16.5 us  [the longest x1 7.41 us: fourier(): pl.pallas_call(functools.partial(fourier_kernel, members, lev_rows, lat_r...]
    convert_element_type x5 -> x0, local copies, waits for them, and re-layouts: 13.5 us -> none  [the longest x2 9.11 us: on_device(): summed = summed_on_arrival(partial_value.astype(jnp.bfloat16), 'lev', 1)]
    all_to_all x5 -> x0, local copies, waits for them, and re-layouts: 13.1 us -> none  [the longest x2 9.36 us: on_device(): lax.all_to_all(lax.all_to_all(slotted, 'lat', split_axis=1, concat_axis=2...]
    select_n x3 -> x0, other arithmetic: 5.56 us -> none  [the longest x1 4.8 us: on_device(): jnp.where(active_flag.reshape(-1)[:, None, None], slotted, jnp.zeros_like...]
  transfers between devices with their start and end apart: 3 -> 0, of which waited for: 3 -> 0; matrix products, arithmetic and copies ran while one was open for 2% -> 0% of each run, Pallas kernels for 0% -> 0%
where the time goes in v1:
time: 130 us
  blocking collectives  107 us (82%)
  Pallas kernels  16.5 us (13%)
  local copies, waits for them, and re-layouts  6.09 us (5%)
    all_to_all x4, blocking collectives, exchange(): return lax.all_to_all(x, axis, split_axis=0, concat_axis=0, tiled=True)  107 us
    pallas_call x1, Pallas kernels, fourier(): pl.pallas_call(functools.partial(fourier_kernel, members, lev_rows, lat_r...  7.41 us
    unnamed x8, local copies, waits for them, and re-layouts  6.09 us
    pallas_call x1, Pallas kernels, legendre_stage(): pl.pallas_call(functools.partial(legendre_kernel, members, lev_rows, lat_...  3.75 us

profile of v1, /device:TPU:1, one launch (start us, length us, event | category | flops | bytes accessed | tf_op | source)
XLA Modules:
  0.0 130.0 jit_solution(13762520522609652673)
XLA Ops:
  0.0 0.0 copy-start
  0.0 2.8 %copy-done = f32[12,16,8,1024]{3,2,1,0:T(8,128)S(1)} copy-done((f32[12,16,8,1024]{3,2,1,0:T(8,128)S(1)}, f32[12,16,8,1024]{3,2,1,0:T(8,128)}, u32[]{:S(2)}) %copy-start) | copy-done | bytes 6291480
  2.8 0.0 copy-start.1
  2.8 1.2 copy-done.1
  4.0 0.0 copy-start.2
  4.0 1.0 copy-done.2
  5.1 0.0 copy-start.3
  5.1 1.0 copy-done.3
  6.1 7.4 %fourier.1 = bf16[2816,384]{1,0:T(8,128)(2,1)S(1)} custom-call(f32[12,128,1024]{2,1,0:T(8,128)S(1)} %bitcast.4, f32[12,128,1024]{2,1,0:T(8,128)S(1)} %bitcast.5, f32[12,128,1024]{2,1,0:T(8,128)S(1)} %bitcast.6, f32[12,128,1024]{2,1,0:T(8,128)S(1)} %bitcast.7, f32[12,128,1024]{2,1,0:T(8,128)S(1)} %bitcast.8, f32[12,128,1024]{2,1,0:T(8,128)S(1)} %bitcast.9, ...), custom_call_target="tpu_custom_call" | custom-call | flops 5000000000 | bytes 10000000 | tf_op jit(solution)/shard_map/fourier/pallas_call | solution.py:109
  13.5 38.0 %all_to_all.20.r_ref = bf16[32,88,384]{2,1,0:T(8,128)(2,1)S(1)} all-to-all(bf16[32,88,384]{2,1,0:T(8,128)(2,1)S(1)} %bitcast.12), channel_id=1, replica_groups=mesh['lat'=32,'lev'=8] {'lat'}, dimensions={0} | all-to-all | bytes 4325376 | tf_op jit(solution)/shard_map/all_to_all | solution.py:308
  51.5 3.7 %legendre.1 = bf16[4096,128]{1,0:T(8,128)(2,1)S(1)} custom-call(bf16[32,88,384]{2,1,0:T(8,128)(2,1)S(1)} %all_to_all.20.r_ref), custom_call_target="tpu_custom_call" | custom-call | flops 2000000000 | bytes 4000000 | tf_op jit(solution)/shard_map/legendre/pallas_call | solution.py:196
  55.2 43.1 %all_to_all.21 = bf16[256,16,128]{2,1,0:T(8,128)(2,1)S(1)} all-to-all(bf16[256,16,128]{2,1,0:T(8,128)(2,1)S(1)} %bitcast.13), channel_id=1, replica_groups=mesh['lat'=32,'lev'=8] {'lat','lev'}, dimensions={0} | all-to-all | bytes 2097152 | tf_op jit(solution)/shard_map/all_to_all | solution.py:308
  98.4 1.7 %covariance.1 = f32[8,32,128]{2,1,0:T(8,128)S(1)} custom-call(bf16[32,8,16,128]{3,2,1,0:T(8,128)(2,1)S(1)} %bitcast.14), custom_call_target="tpu_custom_call" | custom-call | flops 1000000000 | bytes 2000000 | tf_op jit(solution)/shard_map/covariance/pallas_call | solution.py:250
  100.1 11.3 %all_to_all.22.g_ref = f32[8,32,128]{2,1,0:T(8,128)} all-to-all(f32[8,32,128]{2,1,0:T(8,128)S(1)} %covariance.1), channel_id=1, replica_groups=mesh['lat'=32,'lev'=8] {'lev'}, dimensions={0} | all-to-all | bytes 262144 | tf_op jit(solution)/shard_map/all_to_all | solution.py:308
  111.3 1.9 %route.1 = f32[32,16,128]{2,1,0:T(8,128)} custom-call(s32[32]{0:T(128)} %counts_ref.3, f32[8,32,128]{2,1,0:T(8,128)} %all_to_all.22.g_ref), custom_call_target="tpu_custom_call" | custom-call | tf_op jit(solution)/shard_map/route/pallas_call | solution.py:278
  113.3 15.0 %all_to_all.23.r_ref = f32[32,16,128]{2,1,0:T(8,128)} all-to-all(f32[32,16,128]{2,1,0:T(8,128)} %route.1), channel_id=1, replica_groups=mesh['lat'=32,'lev'=8] {'lat'}, dimensions={0} | all-to-all | bytes 524288 | tf_op jit(solution)/shard_map/all_to_all | solution.py:308
  128.3 1.7 %collect.1 = f32[16,16,128]{2,1,0:T(8,128)} custom-call(s32[32]{0:T(128)} %counts_ref.3, f32[32,16,128]{2,1,0:T(8,128)} %all_to_all.23.r_ref), custom_call_target="tpu_custom_call" | custom-call | tf_op jit(solution)/shard_map/collect/pallas_call | solution.py:298
Async XLA Ops:
  0.0 2.8 %copy-start = (f32[12,16,8,1024]{3,2,1,0:T(8,128)S(1)}, f32[12,16,8,1024]{3,2,1,0:T(8,128)}, u32[]{:S(2)}) copy-start(f32[12,16,8,1024]{3,2,1,0:T(8,128)} %param.5) | copy-start | bytes 18874372
  2.8 1.2 copy-start.1
  4.0 1.0 copy-start.2
  5.1 1.0 copy-start.3

commit v2 on v1

--- a/solution.py
+++ b/solution.py
@@ -32,7 +32,7 @@
     table = np.stack(tables)
     high = table.astype(np.float32).astype(ml_dtypes.bfloat16)
     low = (table - high.astype(np.float64)).astype(np.float32).astype(ml_dtypes.bfloat16)
-    return high, low
+    return np.stack([high, low])
 
 
 def dot_nt(a, b):
@@ -47,23 +47,26 @@
     return lax.dot_general(a, b, (((1,), (0,)), ((), ())), preferred_element_type=F32)
 
 
-def fourier_kernel(members, lev_rows, lat_rows, pieces, *refs):
-    f_refs, (leg_ref, hi_ref, lo_ref, out_ref, uhi, ulo, t_ref) = refs[:pieces], refs[pieces:]
-    b = pl.program_id(0)
-    rows = pl.ds(pl.multiple_of(b * lev_rows, lev_rows), lev_rows)
-    for piece in range(pieces // 2):
-        lanes = slice(piece * 128, (piece + 1) * 128)
-        for lat in range(lat_rows):
-            every = pl.ds(lat, lev_rows, stride=lat_rows)
-            left, right = f_refs[piece][0, every, :], f_refs[piece + pieces // 2][0, every, :]
-            for parity, u in enumerate((left + right, left - right)):
-                high = u.astype(BF16)
-                uhi[parity, lat, rows, lanes] = high
-                ulo[parity, lat, rows, lanes] = (u - high.astype(F32)).astype(BF16)
-
-    @pl.when(b < lat_rows)
-    def _():
-        table = leg_ref[0].astype(F32)
+def fourier_kernel(members, lev_rows, lat_rows, f_hbm, leg_hbm, tab_hbm, out_ref, f_ref, leg_ref, tab_ref, uhi, ulo, t_ref, f_sem, sem):
+    pieces = f_ref.shape[0]
+    block_rows = lev_rows * lat_rows
+
+    def fetch(b, piece):
+        rows = pl.ds(pl.multiple_of(b * block_rows, block_rows), block_rows)
+        source = f_hbm.at[b, :, piece * 128 : (piece + 1) * 128]
+        return pltpu.make_async_copy(source, f_ref.at[piece, rows, :], f_sem.at[b, piece])
+
+    leg_copy = pltpu.make_async_copy(leg_hbm, leg_ref, sem.at[0])
+    tab_copy = pltpu.make_async_copy(tab_hbm, tab_ref, sem.at[1])
+    leg_copy.start()
+    for b in range(members):
+        for piece in range(pieces):
+            fetch(b, piece).start()
+    tab_copy.start()
+    leg_copy.wait()
+
+    def pack(lat, carry):
+        table = leg_ref[lat].astype(F32)
         lane = lax.broadcasted_iota(jnp.int32, (STRIDE, 2 * 128), 1)
 
         def block(i):
@@ -77,58 +80,73 @@
         tiles.append(block(BLOCKS // 2)[:, 128:])
         for t, tile in enumerate(tiles):
             first = SPEC_ROWS + (t // 3) * lat_rows
-            t_ref[t % 3, pl.ds(first + b, LATS, stride=ROWS), :] = tile
-
-    @pl.when(b == members - 1)
-    def _():
-        count = LATS // 2 * BLOCKS
-        for lat in range(lat_rows):
-            for parity in range(2):
-                h, l = uhi[parity, lat], ulo[parity, lat]
-                acc = dot_nt(hi_ref[parity], h) + (dot_nt(hi_ref[parity], l) + dot_nt(lo_ref[parity], h))
-                both = jnp.concatenate([acc[:count], acc[count:]], axis=1)
-                for pair in range(LATS // 2):
-                    start = (2 * pair + parity) * ROWS + lat
-                    for t in range(3):
-                        t_ref[t, pl.ds(start, BLOCKS, stride=lat_rows), :] = both[
-                            pair * BLOCKS : (pair + 1) * BLOCKS, t * 128 : (t + 1) * 128
-                        ]
-        for t in range(3):
-            for d in range(LATS):
-                rows = slice(d * ROWS, (d + 1) * ROWS)
-                out_ref[rows, t * 128 : (t + 1) * 128] = t_ref[t, rows, :].astype(BF16)
+            t_ref[t % 3, pl.ds(first + lat, LATS, stride=ROWS), :] = tile
+        return carry
+
+    lax.fori_loop(0, lat_rows, pack, 0)
+
+    def split(b, carry):
+        rows = pl.ds(pl.multiple_of(b * lev_rows, lev_rows), lev_rows)
+        for piece in range(pieces):
+            fetch(b, piece).wait()
+        for piece in range(pieces // 2):
+            lanes = slice(piece * 128, (piece + 1) * 128)
+            for lat in range(lat_rows):
+                every = pl.ds(b * block_rows + lat, lev_rows, stride=lat_rows)
+                left, right = f_ref[piece, every, :], f_ref[piece + pieces // 2, every, :]
+                for parity, u in enumerate((left + right, left - right)):
+                    high = u.astype(BF16)
+                    uhi[parity, lat, rows, lanes] = high
+                    ulo[parity, lat, rows, lanes] = (u - high.astype(F32)).astype(BF16)
+        return carry
+
+    lax.fori_loop(0, members, split, 0)
+    tab_copy.wait()
+    count = LATS // 2 * BLOCKS
+    for lat in range(lat_rows):
+        for parity in range(2):
+            h, l = uhi[parity, lat], ulo[parity, lat]
+            th, tl = tab_ref[0, parity], tab_ref[1, parity]
+            acc = dot_nt(th, h) + (dot_nt(th, l) + dot_nt(tl, h))
+            both = jnp.concatenate([acc[:count], acc[count:]], axis=1)
+            for pair in range(LATS // 2):
+                start = (2 * pair + parity) * ROWS + lat
+                for t in range(3):
+                    t_ref[t, pl.ds(start, BLOCKS, stride=lat_rows), :] = both[
+                        pair * BLOCKS : (pair + 1) * BLOCKS, t * 128 : (t + 1) * 128
+                    ]
+    for t in range(3):
+        for d in range(LATS):
+            rows = slice(d * ROWS, (d + 1) * ROWS)
+            out_ref[rows, t * 128 : (t + 1) * 128] = t_ref[t, rows, :].astype(BF16)
 
 
 def fourier(fields, legendre):
     members, lev_rows, lat_rows, points = fields.shape
     modes = legendre.shape[1]
     columns, pieces = 2 * members * lev_rows, points // 128
-    rows = fields.reshape(members, lev_rows * lat_rows, points)
-    high, low = fourier_tables(points, modes)
-    whole = lambda *shape: pl.BlockSpec(shape, lambda b: (0,) * len(shape))
-    return pl.pallas_call(
-        functools.partial(fourier_kernel, members, lev_rows, lat_rows, pieces),
-        grid=(members,),
-        in_specs=[
-            pl.BlockSpec((1, lev_rows * lat_rows, 128), lambda b, piece=piece: (b, 0, piece))
-            for piece in range(pieces)
-        ]
-        + [
-            pl.BlockSpec((1, modes, modes), lambda b: (jnp.minimum(b, lat_rows - 1), 0, 0)),
-            whole(*high.shape),
-            whole(*low.shape),
-        ],
-        out_specs=whole(LATS * ROWS, columns),
+    tables = fourier_tables(points, modes)
+    split_shape = (2, lat_rows, members * lev_rows, points // 2)
+    hbm = pl.BlockSpec(memory_space=pltpu.HBM)
+    return pl.pallas_call(
+        functools.partial(fourier_kernel, members, lev_rows, lat_rows),
+        in_specs=[hbm, hbm, hbm],
+        out_specs=pl.BlockSpec(memory_space=VMEM),
         out_shape=jax.ShapeDtypeStruct((LATS * ROWS, columns), BF16),
         scratch_shapes=[
-            VMEM((2, lat_rows, members * lev_rows, points // 2), BF16),
-            VMEM((2, lat_rows, members * lev_rows, points // 2), BF16),
+            VMEM((pieces, members * lev_rows * lat_rows, 128), F32),
+            VMEM(legendre.shape, BF16),
+            VMEM(tables.shape, BF16),
+            VMEM(split_shape, BF16),
+            VMEM(split_shape, BF16),
             VMEM((3, LATS * ROWS, 128), F32),
+            pltpu.SemaphoreType.DMA((members, pieces)),
+            pltpu.SemaphoreType.DMA((2,)),
         ],
         compiler_params=pltpu.CompilerParams(vmem_limit_bytes=40 << 20),
         cost_estimate=pl.CostEstimate(flops=5 * 10**9, bytes_accessed=10**7, transcendentals=0),
         name="fourier",
-    )(*[rows] * pieces, legendre, jnp.asarray(high), jnp.asarray(low))
+    )(*[pltpu.with_memory_space_constraint(x, pltpu.HBM) for x in (fields.reshape(members, lev_rows * lat_rows, points), legendre, jnp.asarray(tables))])
 
 
 def place(i, j):
@@ -241,7 +259,7 @@
         two += dot_nn(jnp.where(is_first, zero, turned).astype(BF16), part)
     for s, (total, n) in enumerate(((one, lat + STRIDE * p), (two, lat + STRIDE * (BLOCKS - 1 - p)))):
         divisor = ((members - 1) * (2 * n + 2)).astype(F32)
-        scaled = total / jnp.full((levels, levels), divisor, F32)
+        scaled = (total / jnp.full((levels, levels), divisor, F32)).astype(BF16)
         for v in range(LEVS):
             out_ref[v, s * lev_rows : (s + 1) * lev_rows, :] = scaled[v * lev_rows : (v + 1) * lev_rows]
 
@@ -251,7 +269,7 @@
         functools.partial(covariance_kernel, members, lev_rows),
         in_specs=[pl.BlockSpec(memory_space=VMEM)],
         out_specs=pl.BlockSpec(memory_space=VMEM),
-        out_shape=jax.ShapeDtypeStruct((LEVS, 2 * lev_rows, 128), F32),
+        out_shape=jax.ShapeDtypeStruct((LEVS, 2 * lev_rows, 128), BF16),
         compiler_params=pltpu.CompilerParams(vmem_limit_bytes=40 << 20),
         cost_estimate=pl.CostEstimate(flops=10**9, bytes_accessed=2 * 10**6, transcendentals=0),
         name="covariance",
@@ -264,7 +282,7 @@
     for j in range(BLOCKS):
         p, s = min(j, BLOCKS - 1 - j), int(j >= half)
         rows = slice(s * lev_rows, (s + 1) * lev_rows)
-        f_ref[j] = g_ref[2 * p, rows, :] + g_ref[2 * p + 1, rows, :]
+        f_ref[j] = (g_ref[2 * p, rows, :].astype(F32) + g_ref[2 * p + 1, rows, :].astype(F32)).astype(BF16)
 
     def step(owner, start):
         j = jnp.maximum(start - lat + (STRIDE - 1), 0) // STRIDE
@@ -279,8 +297,9 @@
         functools.partial(route_kernel, lev_rows),
         in_specs=[pl.BlockSpec(memory_space=pltpu.SMEM), pl.BlockSpec(memory_space=VMEM)],
         out_specs=pl.BlockSpec(memory_space=VMEM),
-        out_shape=jax.ShapeDtypeStruct((LATS, lev_rows, 128), F32),
-        scratch_shapes=[VMEM((BLOCKS, lev_rows, 128), F32)],
+        out_shape=jax.ShapeDtypeStruct((LATS, lev_rows, 128), BF16),
+        scratch_shapes=[VMEM((BLOCKS, lev_rows, 128), BF16)],
+        compiler_params=pltpu.CompilerParams(vmem_limit_bytes=8 << 20),
         name="route",
     )(owner_counts, parts)
 
@@ -290,7 +309,7 @@
     start = lax.fori_loop(0, lat, lambda k, s: s + counts_ref[k], jnp.int32(0))
     count = counts_ref[lat]
     for slot in range(out_ref.shape[0]):
-        block = r_ref[(start + slot) % STRIDE]
+        block = r_ref[(start + slot) % STRIDE].astype(F32)
         out_ref[slot] = jnp.where(slot < count, block, jnp.zeros_like(block))
 
 
@@ -300,6 +319,7 @@
         in_specs=[pl.BlockSpec(memory_space=pltpu.SMEM), pl.BlockSpec(memory_space=VMEM)],
         out_specs=pl.BlockSpec(memory_space=VMEM),
         out_shape=jax.ShapeDtypeStruct((capacity, lev_rows, 128), F32),
+        compiler_params=pltpu.CompilerParams(vmem_limit_bytes=8 << 20),
         name="collect",
     )(owner_counts, routed)
 

time: 130 us -> 121 us (0.931)
  local copies, waits for them, and re-layouts: 6.09 us -> 0.01 us
  blocking collectives: 107 us -> 103 us
  Pallas kernels: 16.5 us -> 18.3 us
    unnamed x8 -> x2, local copies, waits for them, and re-layouts: 6.09 us -> 0.01 us
    all_to_all x4, blocking collectives: 107 us -> 103 us  [exchange(): return lax.all_to_all(x, axis, split_axis=0, concat_axis=0, tiled=True)]
    pallas_call x1, Pallas kernels: 7.41 us -> 10.7 us  [fourier(): pl.pallas_call(functools.partial(fourier_kernel, members, lev_rows, lat_r...]
where the time goes in v2:
time: 121 us
  blocking collectives  103 us (85%)
  Pallas kernels  18.3 us (15%)
    all_to_all x4, blocking collectives, exchange(): return lax.all_to_all(x, axis, split_axis=0, concat_axis=0, tiled=True)  103 us
    pallas_call x1, Pallas kernels, fourier(): pl.pallas_call(functools.partial(fourier_kernel, members, lev_rows, lat_r...  10.7 us
    pallas_call x1, Pallas kernels, legendre_stage(): pl.pallas_call(functools.partial(legendre_kernel, members, lev_rows, lat_...  3.76 us

profile of v2, /device:TPU:1, one launch (start us, length us, event | category | flops | bytes accessed | tf_op | source)
XLA Modules:
  0.0 121.2 jit_solution(6962308782529304208)
XLA Ops:
  0.0 10.7 %fourier.1 = bf16[2816,384]{1,0:T(8,128)(2,1)S(1)} custom-call(f32[12,128,1024]{2,1,0:T(8,128)} %bitcast.7, bf16[8,256,256]{2,1,0:T(8,128)(2,1)} %leg_hbm.1, bf16[2,2,256,512]{3,2,1,0:T(8,128)(2,1)} %constant.2.clone.tab_hbm), custom_call_target="tpu_custom_call" | custom-call | flops 5000000000 | bytes 10000000 | tf_op jit(solution)/shard_map/fourier/pallas_call | solution.py:131
  10.7 38.0 %all_to_all.20.r_ref = bf16[32,88,384]{2,1,0:T(8,128)(2,1)S(1)} all-to-all(bf16[32,88,384]{2,1,0:T(8,128)(2,1)S(1)} %bitcast.4), channel_id=1, replica_groups=mesh['lat'=32,'lev'=8] {'lat'}, dimensions={0} | all-to-all | bytes 4325376 | tf_op jit(solution)/shard_map/all_to_all | solution.py:328
  48.6 3.8 %legendre.1 = bf16[4096,128]{1,0:T(8,128)(2,1)S(1)} custom-call(bf16[32,88,384]{2,1,0:T(8,128)(2,1)S(1)} %all_to_all.20.r_ref), custom_call_target="tpu_custom_call" | custom-call | flops 2000000000 | bytes 4000000 | tf_op jit(solution)/shard_map/legendre/pallas_call | solution.py:214
  52.4 43.1 %all_to_all.21 = bf16[256,16,128]{2,1,0:T(8,128)(2,1)S(1)} all-to-all(bf16[256,16,128]{2,1,0:T(8,128)(2,1)S(1)} %bitcast.5), channel_id=1, replica_groups=mesh['lat'=32,'lev'=8] {'lat','lev'}, dimensions={0} | all-to-all | bytes 2097152 | tf_op jit(solution)/shard_map/all_to_all | solution.py:328
  95.5 0.0 copy-start
  95.5 1.7 %covariance.1 = bf16[8,32,128]{2,1,0:T(8,128)(2,1)S(1)} custom-call(bf16[32,8,16,128]{3,2,1,0:T(8,128)(2,1)S(1)} %bitcast.6), custom_call_target="tpu_custom_call" | custom-call | flops 1000000000 | bytes 2000000 | tf_op jit(solution)/shard_map/covariance/pallas_call | solution.py:268
  97.2 9.5 %all_to_all.22.g_ref = bf16[8,32,128]{2,1,0:T(8,128)(2,1)S(1)} all-to-all(bf16[8,32,128]{2,1,0:T(8,128)(2,1)S(1)} %covariance.1), channel_id=1, replica_groups=mesh['lat'=32,'lev'=8] {'lev'}, dimensions={0} | all-to-all | bytes 131072 | tf_op jit(solution)/shard_map/all_to_all | solution.py:328
  106.8 0.0 copy-done
  106.8 0.9 route.1
  107.7 12.3 %all_to_all.23.r_ref = bf16[32,16,128]{2,1,0:T(8,128)(2,1)S(1)} all-to-all(bf16[32,16,128]{2,1,0:T(8,128)(2,1)S(1)} %route.1), channel_id=1, replica_groups=mesh['lat'=32,'lev'=8] {'lat'}, dimensions={0} | all-to-all | bytes 262144 | tf_op jit(solution)/shard_map/all_to_all | solution.py:328
  119.9 1.3 %collect.1 = f32[16,16,128]{2,1,0:T(8,128)} custom-call(s32[32]{0:T(128)S(1)} %copy-done, bf16[32,16,128]{2,1,0:T(8,128)(2,1)S(1)} %all_to_all.23.r_ref), custom_call_target="tpu_custom_call" | custom-call | tf_op jit(solution)/shard_map/collect/pallas_call | solution.py:317
Async XLA Ops:
  95.5 11.3 %copy-start = (s32[32]{0:T(128)S(1)}, s32[32]{0:T(128)}, u32[]{:S(2)}) copy-start(s32[32]{0:T(128)} %counts_ref.3) | copy-start | bytes 388

commit v3 on v2

--- a/solution.py
+++ b/solution.py
@@ -16,7 +16,7 @@
 BLOCKS = 8
 SPEC_ROWS, LEG_ROWS = 64, 24
 ROWS = SPEC_ROWS + LEG_ROWS
-SLOT_ROWS, USED_ROWS = 16, 14
+SLOT_ROWS, USED_ROWS = 14, 14
 VMEM = pltpu.VMEM
 
 
@@ -79,46 +79,49 @@
             tiles += [packed[:, :128], packed[:, 128:]]
         tiles.append(block(BLOCKS // 2)[:, 128:])
         for t, tile in enumerate(tiles):
-            first = SPEC_ROWS + (t // 3) * lat_rows
-            t_ref[t % 3, pl.ds(first + lat, LATS, stride=ROWS), :] = tile
+            first = (t // 3) * lat_rows
+            t_ref[t % 3, pl.ds(first + lat, LATS, stride=LEG_ROWS), :] = tile
         return carry
 
     lax.fori_loop(0, lat_rows, pack, 0)
+    for t in range(3):
+        for d in range(LATS):
+            packed = t_ref[t, d * LEG_ROWS : (d + 1) * LEG_ROWS, :]
+            out_ref[d * ROWS + SPEC_ROWS : (d + 1) * ROWS, t * 128 : (t + 1) * 128] = packed.astype(BF16)
+
+    width = members * lev_rows
 
     def split(b, carry):
-        rows = pl.ds(pl.multiple_of(b * lev_rows, lev_rows), lev_rows)
         for piece in range(pieces):
             fetch(b, piece).wait()
         for piece in range(pieces // 2):
             lanes = slice(piece * 128, (piece + 1) * 128)
             for lat in range(lat_rows):
                 every = pl.ds(b * block_rows + lat, lev_rows, stride=lat_rows)
+                rows = pl.ds(pl.multiple_of(lat * width + b * lev_rows, lev_rows), lev_rows)
                 left, right = f_ref[piece, every, :], f_ref[piece + pieces // 2, every, :]
                 for parity, u in enumerate((left + right, left - right)):
                     high = u.astype(BF16)
-                    uhi[parity, lat, rows, lanes] = high
-                    ulo[parity, lat, rows, lanes] = (u - high.astype(F32)).astype(BF16)
+                    uhi[parity, rows, lanes] = high
+                    ulo[parity, rows, lanes] = (u - high.astype(F32)).astype(BF16)
         return carry
 
     lax.fori_loop(0, members, split, 0)
     tab_copy.wait()
     count = LATS // 2 * BLOCKS
-    for lat in range(lat_rows):
-        for parity in range(2):
-            h, l = uhi[parity, lat], ulo[parity, lat]
-            th, tl = tab_ref[0, parity], tab_ref[1, parity]
+    group = lat_rows // 2
+    for parity in range(2):
+        th, tl = tab_ref[0, parity], tab_ref[1, parity]
+        for g in range(2):
+            columns = slice(g * group * width, (g + 1) * group * width)
+            h, l = uhi[parity, columns], ulo[parity, columns]
             acc = dot_nt(th, h) + (dot_nt(th, l) + dot_nt(tl, h))
-            both = jnp.concatenate([acc[:count], acc[count:]], axis=1)
-            for pair in range(LATS // 2):
-                start = (2 * pair + parity) * ROWS + lat
-                for t in range(3):
-                    t_ref[t, pl.ds(start, BLOCKS, stride=lat_rows), :] = both[
-                        pair * BLOCKS : (pair + 1) * BLOCKS, t * 128 : (t + 1) * 128
-                    ]
-    for t in range(3):
-        for d in range(LATS):
-            rows = slice(d * ROWS, (d + 1) * ROWS)
-            out_ref[rows, t * 128 : (t + 1) * 128] = t_ref[t, rows, :].astype(BF16)
+            for k in range(group):
+                part = acc[:, k * width : (k + 1) * width]
+                both = jnp.concatenate([part[:count], part[count:]], axis=1).astype(BF16)
+                for pair in range(LATS // 2):
+                    start = (2 * pair + parity) * ROWS + (g * group + k) * BLOCKS
+                    out_ref[start : start + BLOCKS, :] = both[pair * BLOCKS : (pair + 1) * BLOCKS]
 
 
 def fourier(fields, legendre):
@@ -126,7 +129,7 @@
     modes = legendre.shape[1]
     columns, pieces = 2 * members * lev_rows, points // 128
     tables = fourier_tables(points, modes)
-    split_shape = (2, lat_rows, members * lev_rows, points // 2)
+    split_shape = (2, lat_rows * members * lev_rows, points // 2)
     hbm = pl.BlockSpec(memory_space=pltpu.HBM)
     return pl.pallas_call(
         functools.partial(fourier_kernel, members, lev_rows, lat_rows),
@@ -139,7 +142,7 @@
             VMEM(tables.shape, BF16),
             VMEM(split_shape, BF16),
             VMEM(split_shape, BF16),
-            VMEM((3, LATS * ROWS, 128), F32),
+            VMEM((3, LATS * LEG_ROWS, 128), F32),
             pltpu.SemaphoreType.DMA((members, pieces)),
             pltpu.SemaphoreType.DMA((2,)),
         ],
@@ -155,9 +158,13 @@
     return [(2 * p + (base + t) // USED_ROWS, (base + t) % USED_ROWS) for t in range(3)]
 
 
-def legendre_kernel(members, lev_rows, lat_rows, r_ref, out_ref, t_ref):
+def legendre_kernel(members, lev_rows, lat_rows, r_ref, out_ref, t_ref, s_ref):
     columns = r_ref.shape[2]
     lats = LATS * lat_rows
+    for t in range(3):
+        for s in range(LATS):
+            rows = slice(s * SPEC_ROWS, (s + 1) * SPEC_ROWS)
+            s_ref[t, rows, :] = r_ref[s, :SPEC_ROWS, t * 128 : (t + 1) * 128].astype(F32)
 
     def rows_of(first, lanes):
         x = r_ref[:, first : first + lat_rows, lanes].astype(F32)
@@ -167,7 +174,8 @@
         return rows_of(SPEC_ROWS + (t // 3) * lat_rows, slice((t % 3) * 128, (t % 3 + 1) * 128))
 
     def spectra(i):
-        return rows_of(i * lat_rows, slice(0, columns))
+        tiles = [s_ref[t, pl.ds(i, lats, stride=BLOCKS), :] for t in range(3)]
+        return jnp.concatenate(tiles, axis=1).astype(BF16)
 
     row = lax.broadcasted_iota(jnp.int32, (columns, columns), 0)
     col = lax.broadcasted_iota(jnp.int32, (columns, columns), 1)
@@ -216,7 +224,7 @@
         in_specs=[pl.BlockSpec(memory_space=VMEM)],
         out_specs=pl.BlockSpec(memory_space=VMEM),
         out_shape=jax.ShapeDtypeStruct((rows, 128), BF16),
-        scratch_shapes=[VMEM((rows, 128), F32)],
+        scratch_shapes=[VMEM((rows, 128), F32), VMEM((3, LATS * SPEC_ROWS, 128), F32)],
         compiler_params=pltpu.CompilerParams(vmem_limit_bytes=40 << 20),
         cost_estimate=pl.CostEstimate(flops=2 * 10**9, bytes_accessed=4 * 10**6, transcendentals=0),
         name="legendre",
@@ -228,12 +236,18 @@
     return p, h
 
 
-def covariance_kernel(members, lev_rows, y_ref, out_ref):
+def covariance_kernel(members, lev_rows, y_ref, out_ref, t_ref):
     levels = LEVS * lev_rows
     count = LATS * SLOT_ROWS
     lev, lat = lax.axis_index("lev"), lax.axis_index("lat")
     p, h = home(lev)
-    parts = [y_ref[:, v].reshape(count, 128) for v in range(LEVS)]
+    step = LEVS * SLOT_ROWS
+    for d in range(LATS):
+        t_ref[d * step : (d + 1) * step, :] = y_ref[d * step : (d + 1) * step, :].astype(F32)
+    parts = []
+    for v in range(LEVS):
+        rows = [t_ref[pl.ds(v * SLOT_ROWS + r, LATS, stride=step), :] for r in range(SLOT_ROWS)]
+        parts.append(jnp.concatenate(rows, axis=0).astype(BF16))
     lane = lax.broadcasted_iota(jnp.int32, (count, 128), 1)
     for bit in (1, 2, 4):
         shift = bit * lev_rows
@@ -247,12 +261,11 @@
             swapped[v | bit] = jnp.where(low, pltpu.roll(a, 128 - shift, 1), b)
         parts = swapped
     first_rows = jnp.where(h == 0, 3 * (p + 1), 0)
-    slot = lax.broadcasted_iota(jnp.int32, (levels, count), 1) % SLOT_ROWS
+    slot = lax.broadcasted_iota(jnp.int32, (levels, count), 1) // LATS
     is_first = slot < first_rows
     one = jnp.zeros((levels, levels), F32)
     two = jnp.zeros((levels, levels), F32)
     for part in parts:
-        part = part.astype(BF16)
         turned = part.astype(F32).T
         zero = jnp.zeros_like(turned)
         one += dot_nn(jnp.where(is_first, turned, zero).astype(BF16), part)
@@ -270,6 +283,7 @@
         in_specs=[pl.BlockSpec(memory_space=VMEM)],
         out_specs=pl.BlockSpec(memory_space=VMEM),
         out_shape=jax.ShapeDtypeStruct((LEVS, 2 * lev_rows, 128), BF16),
+        scratch_shapes=[VMEM(received.shape, F32)],
         compiler_params=pltpu.CompilerParams(vmem_limit_bytes=40 << 20),
         cost_estimate=pl.CostEstimate(flops=10**9, bytes_accessed=2 * 10**6, transcendentals=0),
         name="covariance",
@@ -335,8 +349,8 @@
     first = fourier(fields, legendre)
     first = exchange(first.reshape(LATS, ROWS, -1), "lat")
     second = legendre_stage(first, members, lev_rows, lat_rows)
-    second = exchange(second.reshape(LATS * LEVS, SLOT_ROWS, 128), ("lat", "lev"))
-    third = covariance_stage(second.reshape(LATS, LEVS, SLOT_ROWS, 128), members, lev_rows)
+    second = exchange(second.reshape(LATS * LEVS, SLOT_ROWS // 2, 2, 128), ("lat", "lev"))
+    third = covariance_stage(second.reshape(-1, 128), members, lev_rows)
     third = exchange(third, "lev")
     fourth = route_stage(third, owner_counts, lev_rows)
     fourth = exchange(fourth, "lat")

time: 121 us -> 117 us (0.967)
  blocking collectives: 103 us -> 100 us
    all_to_all x4, blocking collectives: 103 us -> 100 us  [exchange(): return lax.all_to_all(x, axis, split_axis=0, concat_axis=0, tiled=True)]
where the time goes in v3:
time: 117 us
  blocking collectives  100 us (85%)
  Pallas kernels  17.1 us (15%)
    all_to_all x4, blocking collectives, exchange(): return lax.all_to_all(x, axis, split_axis=0, concat_axis=0, tiled=True)  100 us
    pallas_call x1, Pallas kernels, fourier(): pl.pallas_call(functools.partial(fourier_kernel, members, lev_rows, lat_r...  9.51 us
    pallas_call x1, Pallas kernels, legendre_stage(): pl.pallas_call(functools.partial(legendre_kernel, members, lev_rows, lat_...  3.22 us

profile of v3, /device:TPU:1, one launch (start us, length us, event | category | flops | bytes accessed | tf_op | source)
XLA Modules:
  0.0 117.2 jit_solution(2955204696841381331)
XLA Ops:
  0.0 9.5 %fourier.1 = bf16[2816,384]{1,0:T(8,128)(2,1)S(1)} custom-call(f32[12,128,1024]{2,1,0:T(8,128)} %bitcast.7, bf16[8,256,256]{2,1,0:T(8,128)(2,1)} %leg_hbm.1, bf16[2,2,256,512]{3,2,1,0:T(8,128)(2,1)} %constant.2.clone.tab_hbm), custom_call_target="tpu_custom_call" | custom-call | flops 5000000000 | bytes 10000000 | tf_op jit(solution)/shard_map/fourier/pallas_call | solution.py:134
  9.5 38.0 %all_to_all.20.r_ref = bf16[32,88,384]{2,1,0:T(8,128)(2,1)S(1)} all-to-all(bf16[32,88,384]{2,1,0:T(8,128)(2,1)S(1)} %bitcast.4), channel_id=1, replica_groups=mesh['lat'=32,'lev'=8] {'lat'}, dimensions={0} | all-to-all | bytes 4325376 | tf_op jit(solution)/shard_map/all_to_all | solution.py:342
  47.5 3.2 %legendre.1 = bf16[3584,128]{1,0:T(8,128)(2,1)S(1)} custom-call(bf16[32,88,384]{2,1,0:T(8,128)(2,1)S(1)} %all_to_all.20.r_ref), custom_call_target="tpu_custom_call" | custom-call | flops 2000000000 | bytes 4000000 | tf_op jit(solution)/shard_map/legendre/pallas_call | solution.py:222
  50.7 40.4 %all_to_all.21 = bf16[256,7,2,128]{3,2,1,0:T(2,128)(2,1)S(1)} all-to-all(bf16[256,7,2,128]{3,2,1,0:T(2,128)(2,1)S(1)} %bitcast.5), channel_id=1, replica_groups=mesh['lat'=32,'lev'=8] {'lat','lev'}, dimensions={0} | all-to-all | bytes 1835008 | tf_op jit(solution)/shard_map/all_to_all | solution.py:342
  91.1 0.0 copy-start
  91.1 2.2 %covariance.1 = bf16[8,32,128]{2,1,0:T(8,128)(2,1)S(1)} custom-call(bf16[3584,128]{1,0:T(8,128)(2,1)S(1)} %bitcast.6), custom_call_target="tpu_custom_call" | custom-call | flops 1000000000 | bytes 2000000 | tf_op jit(solution)/shard_map/covariance/pallas_call | solution.py:281
  93.3 9.5 %all_to_all.22.g_ref = bf16[8,32,128]{2,1,0:T(8,128)(2,1)S(1)} all-to-all(bf16[8,32,128]{2,1,0:T(8,128)(2,1)S(1)} %covariance.1), channel_id=1, replica_groups=mesh['lat'=32,'lev'=8] {'lev'}, dimensions={0} | all-to-all | bytes 131072 | tf_op jit(solution)/shard_map/all_to_all | solution.py:342
  102.8 0.0 copy-done
  102.8 0.9 route.1
  103.7 12.2 %all_to_all.23.r_ref = bf16[32,16,128]{2,1,0:T(8,128)(2,1)S(1)} all-to-all(bf16[32,16,128]{2,1,0:T(8,128)(2,1)S(1)} %route.1), channel_id=1, replica_groups=mesh['lat'=32,'lev'=8] {'lat'}, dimensions={0} | all-to-all | bytes 262144 | tf_op jit(solution)/shard_map/all_to_all | solution.py:342
  115.9 1.3 %collect.1 = f32[16,16,128]{2,1,0:T(8,128)} custom-call(s32[32]{0:T(128)S(1)} %copy-done, bf16[32,16,128]{2,1,0:T(8,128)(2,1)S(1)} %all_to_all.23.r_ref), custom_call_target="tpu_custom_call" | custom-call | tf_op jit(solution)/shard_map/collect/pallas_call | solution.py:331
Async XLA Ops:
  91.1 11.7 %copy-start = (s32[32]{0:T(128)S(1)}, s32[32]{0:T(128)}, u32[]{:S(2)}) copy-start(s32[32]{0:T(128)} %counts_ref.3) | copy-start | bytes 388

commit v4 on v3

--- a/solution.py
+++ b/solution.py
@@ -58,14 +58,13 @@
 
     leg_copy = pltpu.make_async_copy(leg_hbm, leg_ref, sem.at[0])
     tab_copy = pltpu.make_async_copy(tab_hbm, tab_ref, sem.at[1])
-    leg_copy.start()
     for b in range(members):
         for piece in range(pieces):
             fetch(b, piece).start()
     tab_copy.start()
-    leg_copy.wait()
-
-    def pack(lat, carry):
+    leg_copy.start()
+
+    def pack(lat):
         table = leg_ref[lat].astype(F32)
         lane = lax.broadcasted_iota(jnp.int32, (STRIDE, 2 * 128), 1)
 
@@ -81,13 +80,6 @@
         for t, tile in enumerate(tiles):
             first = (t // 3) * lat_rows
             t_ref[t % 3, pl.ds(first + lat, LATS, stride=LEG_ROWS), :] = tile
-        return carry
-
-    lax.fori_loop(0, lat_rows, pack, 0)
-    for t in range(3):
-        for d in range(LATS):
-            packed = t_ref[t, d * LEG_ROWS : (d + 1) * LEG_ROWS, :]
-            out_ref[d * ROWS + SPEC_ROWS : (d + 1) * ROWS, t * 128 : (t + 1) * 128] = packed.astype(BF16)
 
     width = members * lev_rows
 
@@ -108,11 +100,14 @@
 
     lax.fori_loop(0, members, split, 0)
     tab_copy.wait()
+    leg_copy.wait()
     count = LATS // 2 * BLOCKS
     group = lat_rows // 2
     for parity in range(2):
         th, tl = tab_ref[0, parity], tab_ref[1, parity]
         for g in range(2):
+            for k in range(lat_rows // 4):
+                pack((2 * parity + g) * (lat_rows // 4) + k)
             columns = slice(g * group * width, (g + 1) * group * width)
             h, l = uhi[parity, columns], ulo[parity, columns]
             acc = dot_nt(th, h) + (dot_nt(th, l) + dot_nt(tl, h))
@@ -122,6 +117,10 @@
                 for pair in range(LATS // 2):
                     start = (2 * pair + parity) * ROWS + (g * group + k) * BLOCKS
                     out_ref[start : start + BLOCKS, :] = both[pair * BLOCKS : (pair + 1) * BLOCKS]
+    for t in range(3):
+        for d in range(LATS):
+            packed = t_ref[t, d * LEG_ROWS : (d + 1) * LEG_ROWS, :]
+            out_ref[d * ROWS + SPEC_ROWS : (d + 1) * ROWS, t * 128 : (t + 1) * 128] = packed.astype(BF16)
 
 
 def fourier(fields, legendre):
@@ -186,7 +185,7 @@
     zero = jnp.zeros((LATS, 128), F32)
     for k in range(2 * BLOCKS // 2):
         for r in range(USED_ROWS - (k % 2), SLOT_ROWS):
-            t_ref[pl.ds(k * SLOT_ROWS + r, LATS, stride=LEVS * SLOT_ROWS), :] = zero
+            t_ref[pl.ds(k * LATS * SLOT_ROWS + r, LATS, stride=SLOT_ROWS), :] = zero
 
     def finish(waves, units):
         high = waves.astype(BF16)
@@ -195,7 +194,7 @@
         anomaly = waves - total * (1.0 / members)
         for u, (i, j) in enumerate(units):
             for t, (k, r) in enumerate(place(i, j)):
-                t_ref[pl.ds(k * SLOT_ROWS + r, LATS, stride=LEVS * SLOT_ROWS), :] = anomaly[
+                t_ref[pl.ds(k * LATS * SLOT_ROWS + r, LATS, stride=SLOT_ROWS), :] = anomaly[
                     u * STRIDE : (u + 1) * STRIDE, t * 128 : (t + 1) * 128
                 ]
 
@@ -212,9 +211,9 @@
         finish(upper, units[4:])
     p = BLOCKS // 2
     finish(dot_tn(table(2 * p), spectra(p)), [(p, j) for j in range(p, BLOCKS)])
-    step = LEVS * SLOT_ROWS
-    for c in range(LATS):
-        out_ref[c * step : (c + 1) * step, :] = t_ref[c * step : (c + 1) * step, :].astype(BF16)
+    step = LATS * SLOT_ROWS
+    for k in range(LEVS):
+        out_ref[k * step : (k + 1) * step, :] = t_ref[k * step : (k + 1) * step, :].astype(BF16)
 
 
 def legendre_stage(received, members, lev_rows, lat_rows):
@@ -236,18 +235,12 @@
     return p, h
 
 
-def covariance_kernel(members, lev_rows, y_ref, out_ref, t_ref):
+def covariance_kernel(members, lev_rows, y_ref, out_ref):
     levels = LEVS * lev_rows
     count = LATS * SLOT_ROWS
     lev, lat = lax.axis_index("lev"), lax.axis_index("lat")
     p, h = home(lev)
-    step = LEVS * SLOT_ROWS
-    for d in range(LATS):
-        t_ref[d * step : (d + 1) * step, :] = y_ref[d * step : (d + 1) * step, :].astype(F32)
-    parts = []
-    for v in range(LEVS):
-        rows = [t_ref[pl.ds(v * SLOT_ROWS + r, LATS, stride=step), :] for r in range(SLOT_ROWS)]
-        parts.append(jnp.concatenate(rows, axis=0).astype(BF16))
+    parts = [y_ref[v * count : (v + 1) * count, :] for v in range(LEVS)]
     lane = lax.broadcasted_iota(jnp.int32, (count, 128), 1)
     for bit in (1, 2, 4):
         shift = bit * lev_rows
@@ -261,7 +254,7 @@
             swapped[v | bit] = jnp.where(low, pltpu.roll(a, 128 - shift, 1), b)
         parts = swapped
     first_rows = jnp.where(h == 0, 3 * (p + 1), 0)
-    slot = lax.broadcasted_iota(jnp.int32, (levels, count), 1) // LATS
+    slot = lax.broadcasted_iota(jnp.int32, (levels, count), 1) % SLOT_ROWS
     is_first = slot < first_rows
     one = jnp.zeros((levels, levels), F32)
     two = jnp.zeros((levels, levels), F32)
@@ -283,7 +276,6 @@
         in_specs=[pl.BlockSpec(memory_space=VMEM)],
         out_specs=pl.BlockSpec(memory_space=VMEM),
         out_shape=jax.ShapeDtypeStruct((LEVS, 2 * lev_rows, 128), BF16),
-        scratch_shapes=[VMEM(received.shape, F32)],
         compiler_params=pltpu.CompilerParams(vmem_limit_bytes=40 << 20),
         cost_estimate=pl.CostEstimate(flops=10**9, bytes_accessed=2 * 10**6, transcendentals=0),
         name="covariance",
@@ -349,7 +341,7 @@
     first = fourier(fields, legendre)
     first = exchange(first.reshape(LATS, ROWS, -1), "lat")
     second = legendre_stage(first, members, lev_rows, lat_rows)
-    second = exchange(second.reshape(LATS * LEVS, SLOT_ROWS // 2, 2, 128), ("lat", "lev"))
+    second = exchange(second.reshape(LATS * LEVS, SLOT_ROWS // 2, 2, 128), ("lev", "lat"))
     third = covariance_stage(second.reshape(-1, 128), members, lev_rows)
     third = exchange(third, "lev")
     fourth = route_stage(third, owner_counts, lev_rows)

time: 117 us -> 115 us (0.983)
  Pallas kernels: 17.1 us -> 14.4 us
    pallas_call x1, Pallas kernels: 9.51 us -> 7.42 us  [fourier(): pl.pallas_call(functools.partial(fourier_kernel, members, lev_rows, lat_r...]
where the time goes in v4:
time: 115 us; the launch traced here: 114 us
  blocking collectives  100 us (87%)
  Pallas kernels  14.4 us (13%)
    all_to_all x4, blocking collectives, exchange(): return lax.all_to_all(x, axis, split_axis=0, concat_axis=0, tiled=True)  100 us
    pallas_call x1, Pallas kernels, fourier(): pl.pallas_call(functools.partial(fourier_kernel, members, lev_rows, lat_r...  7.42 us
    pallas_call x1, Pallas kernels, legendre_stage(): pl.pallas_call(functools.partial(legendre_kernel, members, lev_rows, lat_...  2.99 us

profile of v4, /device:TPU:1, one launch (start us, length us, event | category | flops | bytes accessed | tf_op | source)
XLA Modules:
  0.0 114.4 jit_solution(11144186177809573184)
XLA Ops:
  0.0 7.4 %fourier.1 = bf16[2816,384]{1,0:T(8,128)(2,1)S(1)} custom-call(f32[12,128,1024]{2,1,0:T(8,128)} %bitcast.7, bf16[8,256,256]{2,1,0:T(8,128)(2,1)} %leg_hbm.1, bf16[2,2,256,512]{3,2,1,0:T(8,128)(2,1)} %constant.2.clone.tab_hbm), custom_call_target="tpu_custom_call" | custom-call | flops 5000000000 | bytes 10000000 | tf_op jit(solution)/shard_map/fourier/pallas_call | solution.py:133
  7.4 38.0 %all_to_all.20.r_ref = bf16[32,88,384]{2,1,0:T(8,128)(2,1)S(1)} all-to-all(bf16[32,88,384]{2,1,0:T(8,128)(2,1)S(1)} %bitcast.4), channel_id=1, replica_groups=mesh['lat'=32,'lev'=8] {'lat'}, dimensions={0} | all-to-all | bytes 4325376 | tf_op jit(solution)/shard_map/all_to_all | solution.py:334
  45.4 3.0 %legendre.1 = bf16[3584,128]{1,0:T(8,128)(2,1)S(1)} custom-call(bf16[32,88,384]{2,1,0:T(8,128)(2,1)S(1)} %all_to_all.20.r_ref), custom_call_target="tpu_custom_call" | custom-call | flops 2000000000 | bytes 4000000 | tf_op jit(solution)/shard_map/legendre/pallas_call | solution.py:221
  48.4 38.4 %all_to_all.21 = bf16[256,7,2,128]{3,2,1,0:T(2,128)(2,1)S(1)} all-to-all(bf16[256,7,2,128]{3,2,1,0:T(2,128)(2,1)S(1)} %bitcast.5), channel_id=1, replica_groups=mesh['lat'=32,'lev'=8] {'lev','lat'}, dimensions={0} | all-to-all | bytes 1835008 | tf_op jit(solution)/shard_map/all_to_all | solution.py:334
  86.8 0.0 copy-start
  86.8 1.8 %covariance.1 = bf16[8,32,128]{2,1,0:T(8,128)(2,1)S(1)} custom-call(bf16[3584,128]{1,0:T(8,128)(2,1)S(1)} %bitcast.6), custom_call_target="tpu_custom_call" | custom-call | flops 1000000000 | bytes 2000000 | tf_op jit(solution)/shard_map/covariance/pallas_call | solution.py:274
  88.6 11.1 %all_to_all.22.g_ref = bf16[8,32,128]{2,1,0:T(8,128)(2,1)S(1)} all-to-all(bf16[8,32,128]{2,1,0:T(8,128)(2,1)S(1)} %covariance.1), channel_id=1, replica_groups=mesh['lat'=32,'lev'=8] {'lev'}, dimensions={0} | all-to-all | bytes 131072 | tf_op jit(solution)/shard_map/all_to_all | solution.py:334
  99.7 0.0 copy-done
  99.7 0.9 route.1
  100.6 12.5 %all_to_all.23.r_ref = bf16[32,16,128]{2,1,0:T(8,128)(2,1)S(1)} all-to-all(bf16[32,16,128]{2,1,0:T(8,128)(2,1)S(1)} %route.1), channel_id=1, replica_groups=mesh['lat'=32,'lev'=8] {'lat'}, dimensions={0} | all-to-all | bytes 262144 | tf_op jit(solution)/shard_map/all_to_all | solution.py:334
  113.1 1.3 %collect.1 = f32[16,16,128]{2,1,0:T(8,128)} custom-call(s32[32]{0:T(128)S(1)} %copy-done, bf16[32,16,128]{2,1,0:T(8,128)(2,1)S(1)} %all_to_all.23.r_ref), custom_call_target="tpu_custom_call" | custom-call | tf_op jit(solution)/shard_map/collect/pallas_call | solution.py:323
Async XLA Ops:
  86.8 12.9 %copy-start = (s32[32]{0:T(128)S(1)}, s32[32]{0:T(128)}, u32[]{:S(2)}) copy-start(s32[32]{0:T(128)} %counts_ref.3) | copy-start | bytes 388

commit v5 on v4

--- a/solution.py
+++ b/solution.py
@@ -17,22 +17,21 @@
 SPEC_ROWS, LEG_ROWS = 64, 24
 ROWS = SPEC_ROWS + LEG_ROWS
 SLOT_ROWS, USED_ROWS = 14, 14
+CLASSES = ((0, 4, 4), (2, 4, 4), (1, 2, 2))
 VMEM = pltpu.VMEM
 
 
 def fourier_tables(points, modes):
-    half = points // 2
-    j = np.arange(half)
     tables = []
-    for parity in range(2):
-        d = 2 * np.arange(LATS // 2) + parity
-        m = (d[:, None] + STRIDE * np.arange(BLOCKS)[None, :]).reshape(-1)
+    for first, step, fold in CLASSES:
+        j = np.arange(points // fold)
+        m = (np.arange(first, LATS, step)[:, None] + STRIDE * np.arange(BLOCKS)[None, :]).reshape(-1)
         angle = (m[:, None] * j[None, :] % points) * (2.0 * math.pi / points)
-        tables.append(np.concatenate([np.cos(angle), -np.sin(angle)]) * points**-0.5)
-    table = np.stack(tables)
-    high = table.astype(np.float32).astype(ml_dtypes.bfloat16)
-    low = (table - high.astype(np.float64)).astype(np.float32).astype(ml_dtypes.bfloat16)
-    return np.stack([high, low])
+        table = np.concatenate([np.cos(angle), -np.sin(angle)]) * points**-0.5
+        high = table.astype(np.float32).astype(ml_dtypes.bfloat16)
+        low = (table - high.astype(np.float64)).astype(np.float32).astype(ml_dtypes.bfloat16)
+        tables.append(np.concatenate([high, low]))
+    return tables
 
 
 def dot_nt(a, b):
@@ -47,7 +46,11 @@
     return lax.dot_general(a, b, (((1,), (0,)), ((), ())), preferred_element_type=F32)
 
 
-def fourier_kernel(members, lev_rows, lat_rows, f_hbm, leg_hbm, tab_hbm, out_ref, f_ref, leg_ref, tab_ref, uhi, ulo, t_ref, f_sem, sem):
+def fourier_kernel(members, lev_rows, lat_rows, f_hbm, leg_hbm, *refs):
+    classes = len(CLASSES)
+    tab_hbm, (out_ref, f_ref, leg_ref), refs = refs[:classes], refs[classes : classes + 3], refs[classes + 3 :]
+    tab_refs, high_refs, low_refs = refs[:classes], refs[classes : 2 * classes], refs[2 * classes : 3 * classes]
+    t_ref, f_sem, sem = refs[3 * classes :]
     pieces = f_ref.shape[0]
     block_rows = lev_rows * lat_rows
 
@@ -56,12 +59,13 @@
         source = f_hbm.at[b, :, piece * 128 : (piece + 1) * 128]
         return pltpu.make_async_copy(source, f_ref.at[piece, rows, :], f_sem.at[b, piece])
 
-    leg_copy = pltpu.make_async_copy(leg_hbm, leg_ref, sem.at[0])
-    tab_copy = pltpu.make_async_copy(tab_hbm, tab_ref, sem.at[1])
+    leg_copy = pltpu.make_async_copy(leg_hbm, leg_ref, sem.at[classes])
+    tab_copies = [pltpu.make_async_copy(tab_hbm[c], tab_refs[c], sem.at[c]) for c in range(classes)]
     for b in range(members):
         for piece in range(pieces):
             fetch(b, piece).start()
-    tab_copy.start()
+    for copy in tab_copies:
+        copy.start()
     leg_copy.start()
 
     def pack(lat):
@@ -81,42 +85,66 @@
             first = (t // 3) * lat_rows
             t_ref[t % 3, pl.ds(first + lat, LATS, stride=LEG_ROWS), :] = tile
 
-    width = members * lev_rows
+    group = lat_rows // 2
+    main = 128 // lev_rows
+    rest = members - main
+    width = group * members * lev_rows
 
     def split(b, carry):
         for piece in range(pieces):
             fetch(b, piece).wait()
-        for piece in range(pieces // 2):
-            lanes = slice(piece * 128, (piece + 1) * 128)
-            for lat in range(lat_rows):
-                every = pl.ds(b * block_rows + lat, lev_rows, stride=lat_rows)
-                rows = pl.ds(pl.multiple_of(lat * width + b * lev_rows, lev_rows), lev_rows)
-                left, right = f_ref[piece, every, :], f_ref[piece + pieces // 2, every, :]
-                for parity, u in enumerate((left + right, left - right)):
-                    high = u.astype(BF16)
-                    uhi[parity, rows, lanes] = high
-                    ulo[parity, rows, lanes] = (u - high.astype(F32)).astype(BF16)
+        for lat in range(lat_rows):
+            every = pl.ds(b * block_rows + lat, lev_rows, stride=lat_rows)
+            k = lat % group
+            inside = jnp.where(b < main, k * 128 + b * lev_rows, group * 128 + (k * rest + b - main) * lev_rows)
+            rows = pl.ds(pl.multiple_of(lat // group * width + inside, lev_rows), lev_rows)
+
+            def store(c, piece, u):
+                lanes = slice(piece * 128, (piece + 1) * 128)
+                high = u.astype(BF16)
+                high_refs[c][rows, lanes] = high
+                low_refs[c][rows, lanes] = (u - high.astype(F32)).astype(BF16)
+
+            quarter = pieces // 4
+            for piece in range(quarter):
+                x0, x1, x2, x3 = [f_ref[piece + q * quarter, every, :] for q in range(4)]
+                even, odd = x0 + x2, x1 + x3
+                store(0, piece, even + odd)
+                store(1, piece, even - odd)
+                store(2, piece, x0 - x2)
+                store(2, piece + quarter, x1 - x3)
         return carry
 
     lax.fori_loop(0, members, split, 0)
-    tab_copy.wait()
+    for copy in tab_copies:
+        copy.wait()
     leg_copy.wait()
-    count = LATS // 2 * BLOCKS
-    group = lat_rows // 2
-    for parity in range(2):
-        th, tl = tab_ref[0, parity], tab_ref[1, parity]
-        for g in range(2):
-            for k in range(lat_rows // 4):
-                pack((2 * parity + g) * (lat_rows // 4) + k)
-            columns = slice(g * group * width, (g + 1) * group * width)
-            h, l = uhi[parity, columns], ulo[parity, columns]
-            acc = dot_nt(th, h) + (dot_nt(th, l) + dot_nt(tl, h))
+    waiting = list(range(lat_rows))
+    for g in range(2):
+        columns = slice(g * width, (g + 1) * width)
+        for c, (first, step, fold) in enumerate(CLASSES):
+            for k in range(2 if fold == 2 else 1):
+                pack(waiting.pop())
+            tab, h, l = tab_refs[c][...], high_refs[c][columns], low_refs[c][columns]
+            double = tab.shape[0] // 2
+            products = dot_nt(tab, h)
+            acc = products[:double] + (products[double:] + dot_nt(tab[:double], l))
+            count = double // 2
+            lane = lax.broadcasted_iota(jnp.int32, (count, 128), 1)
             for k in range(group):
-                part = acc[:, k * width : (k + 1) * width]
-                both = jnp.concatenate([part[:count], part[count:]], axis=1).astype(BF16)
-                for pair in range(LATS // 2):
-                    start = (2 * pair + parity) * ROWS + (g * group + k) * BLOCKS
-                    out_ref[start : start + BLOCKS, :] = both[pair * BLOCKS : (pair + 1) * BLOCKS]
+                here = slice(k * 128, (k + 1) * 128)
+                tail = slice((group + k // 2) * 128, (group + k // 2 + 1) * 128)
+                cos_tail, sin_tail = acc[:count, tail], acc[count:, tail]
+                if k % 2 == 0:
+                    sin_tail = pltpu.roll(sin_tail, 64, 1)
+                else:
+                    cos_tail = pltpu.roll(cos_tail, 64, 1)
+                middle = jnp.where(lane < 64, cos_tail, sin_tail)
+                for t, tile in enumerate((acc[:count, here], middle, acc[count:, here])):
+                    tile = tile.astype(BF16)
+                    for n in range(count // BLOCKS):
+                        start = (first + step * n) * ROWS + (g * group + k) * BLOCKS
+                        out_ref[start : start + BLOCKS, t * 128 : (t + 1) * 128] = tile[n * BLOCKS : (n + 1) * BLOCKS]
     for t in range(3):
         for d in range(LATS):
             packed = t_ref[t, d * LEG_ROWS : (d + 1) * LEG_ROWS, :]
@@ -128,27 +156,27 @@
     modes = legendre.shape[1]
     columns, pieces = 2 * members * lev_rows, points // 128
     tables = fourier_tables(points, modes)
-    split_shape = (2, lat_rows * members * lev_rows, points // 2)
-    hbm = pl.BlockSpec(memory_space=pltpu.HBM)
+    splits = [VMEM((lat_rows * members * lev_rows, table.shape[1]), BF16) for table in tables]
+    operands = [fields.reshape(members, lev_rows * lat_rows, points), legendre] + [jnp.asarray(t) for t in tables]
     return pl.pallas_call(
         functools.partial(fourier_kernel, members, lev_rows, lat_rows),
-        in_specs=[hbm, hbm, hbm],
+        in_specs=[pl.BlockSpec(memory_space=pltpu.HBM)] * len(operands),
         out_specs=pl.BlockSpec(memory_space=VMEM),
         out_shape=jax.ShapeDtypeStruct((LATS * ROWS, columns), BF16),
         scratch_shapes=[
             VMEM((pieces, members * lev_rows * lat_rows, 128), F32),
             VMEM(legendre.shape, BF16),
-            VMEM(tables.shape, BF16),
-            VMEM(split_shape, BF16),
-            VMEM(split_shape, BF16),
+            *[VMEM(table.shape, BF16) for table in tables],
+            *splits,
+            *splits,
             VMEM((3, LATS * LEG_ROWS, 128), F32),
             pltpu.SemaphoreType.DMA((members, pieces)),
-            pltpu.SemaphoreType.DMA((2,)),
+            pltpu.SemaphoreType.DMA((len(tables) + 1,)),
         ],
         compiler_params=pltpu.CompilerParams(vmem_limit_bytes=40 << 20),
         cost_estimate=pl.CostEstimate(flops=5 * 10**9, bytes_accessed=10**7, transcendentals=0),
         name="fourier",
-    )(*[pltpu.with_memory_space_constraint(x, pltpu.HBM) for x in (fields.reshape(members, lev_rows * lat_rows, points), legendre, jnp.asarray(tables))])
+    )(*[pltpu.with_memory_space_constraint(x, pltpu.HBM) for x in operands])
 
 
 def place(i, j):

time: 115 us -> 114 us (level)
  no operation moved by 1% of the time
where the time goes in v5:
time: 114 us
  blocking collectives  100 us (88%)
  Pallas kernels  14 us (12%)
    all_to_all x4, blocking collectives, exchange(): return lax.all_to_all(x, axis, split_axis=0, concat_axis=0, tiled=True)  100 us
    pallas_call x1, Pallas kernels, fourier(): pl.pallas_call(functools.partial(fourier_kernel, members, lev_rows, lat_r...  7.03 us
    pallas_call x1, Pallas kernels, legendre_stage(): pl.pallas_call(functools.partial(legendre_kernel, members, lev_rows, lat_...  2.98 us

profile of v5, /device:TPU:1, one launch (start us, length us, event | category | flops | bytes accessed | tf_op | source)
XLA Modules:
  0.0 114.0 jit_solution(424329641386628999)
XLA Ops:
  0.0 7.0 %fourier.1 = bf16[2816,384]{1,0:T(8,128)(2,1)S(1)} custom-call(f32[12,128,1024]{2,1,0:T(8,128)} %bitcast.7, bf16[8,256,256]{2,1,0:T(8,128)(2,1)} %leg_hbm.1, bf16[256,256]{1,0:T(8,128)(2,1)} %constant.6.clone.refs_0_, bf16[256,256]{1,0:T(8,128)(2,1)} %constant.7.clone.refs_1_, bf16[512,512]{1,0:T(8,128)(2,1)} %constant.8.clone.refs_2_), custom_call_target="tpu_custom_call" | custom-call | flops 5000000000 | bytes 10000000 | tf_op jit(solution)/shard_map/fourier/pallas_call | solution.py:161
  7.0 38.0 %all_to_all.20.r_ref = bf16[32,88,384]{2,1,0:T(8,128)(2,1)S(1)} all-to-all(bf16[32,88,384]{2,1,0:T(8,128)(2,1)S(1)} %bitcast.4), channel_id=1, replica_groups=mesh['lat'=32,'lev'=8] {'lat'}, dimensions={0} | all-to-all | bytes 4325376 | tf_op jit(solution)/shard_map/all_to_all | solution.py:362
  45.0 3.0 %legendre.1 = bf16[3584,128]{1,0:T(8,128)(2,1)S(1)} custom-call(bf16[32,88,384]{2,1,0:T(8,128)(2,1)S(1)} %all_to_all.20.r_ref), custom_call_target="tpu_custom_call" | custom-call | flops 2000000000 | bytes 4000000 | tf_op jit(solution)/shard_map/legendre/pallas_call | solution.py:249
  48.0 38.4 %all_to_all.21 = bf16[256,7,2,128]{3,2,1,0:T(2,128)(2,1)S(1)} all-to-all(bf16[256,7,2,128]{3,2,1,0:T(2,128)(2,1)S(1)} %bitcast.5), channel_id=1, replica_groups=mesh['lat'=32,'lev'=8] {'lev','lat'}, dimensions={0} | all-to-all | bytes 1835008 | tf_op jit(solution)/shard_map/all_to_all | solution.py:362
  86.4 0.0 copy-start
  86.4 1.8 %covariance.1 = bf16[8,32,128]{2,1,0:T(8,128)(2,1)S(1)} custom-call(bf16[3584,128]{1,0:T(8,128)(2,1)S(1)} %bitcast.6), custom_call_target="tpu_custom_call" | custom-call | flops 1000000000 | bytes 2000000 | tf_op jit(solution)/shard_map/covariance/pallas_call | solution.py:302
  88.2 11.1 %all_to_all.22.g_ref = bf16[8,32,128]{2,1,0:T(8,128)(2,1)S(1)} all-to-all(bf16[8,32,128]{2,1,0:T(8,128)(2,1)S(1)} %covariance.1), channel_id=1, replica_groups=mesh['lat'=32,'lev'=8] {'lev'}, dimensions={0} | all-to-all | bytes 131072 | tf_op jit(solution)/shard_map/all_to_all | solution.py:362
  99.3 0.0 copy-done
  99.3 0.9 route.1
  100.2 12.5 %all_to_all.23.r_ref = bf16[32,16,128]{2,1,0:T(8,128)(2,1)S(1)} all-to-all(bf16[32,16,128]{2,1,0:T(8,128)(2,1)S(1)} %route.1), channel_id=1, replica_groups=mesh['lat'=32,'lev'=8] {'lat'}, dimensions={0} | all-to-all | bytes 262144 | tf_op jit(solution)/shard_map/all_to_all | solution.py:362
  112.7 1.3 %collect.1 = f32[16,16,128]{2,1,0:T(8,128)} custom-call(s32[32]{0:T(128)S(1)} %copy-done, bf16[32,16,128]{2,1,0:T(8,128)(2,1)S(1)} %all_to_all.23.r_ref), custom_call_target="tpu_custom_call" | custom-call | tf_op jit(solution)/shard_map/collect/pallas_call | solution.py:351
Async XLA Ops:
  86.4 12.9 %copy-start = (s32[32]{0:T(128)S(1)}, s32[32]{0:T(128)}, u32[]{:S(2)}) copy-start(s32[32]{0:T(128)} %counts_ref.3) | copy-start | bytes 388

commit v6 on v5

--- a/solution.py
+++ b/solution.py
@@ -204,10 +204,9 @@
         tiles = [s_ref[t, pl.ds(i, lats, stride=BLOCKS), :] for t in range(3)]
         return jnp.concatenate(tiles, axis=1).astype(BF16)
 
-    row = lax.broadcasted_iota(jnp.int32, (columns, columns), 0)
-    col = lax.broadcasted_iota(jnp.int32, (columns, columns), 1)
-    half = members * lev_rows
-    same = ((row >= half) == (col >= half)) & (row % lev_rows == col % lev_rows)
+    row = lax.broadcasted_iota(jnp.int32, (256, 256), 0)
+    col = lax.broadcasted_iota(jnp.int32, (256, 256), 1)
+    same = ((row >= 128) == (col >= 128)) & (row % lev_rows == col % lev_rows)
     ones = jnp.where(same, 1.0, 0.0).astype(BF16)
 
     zero = jnp.zeros((LATS, 128), F32)
@@ -216,10 +215,17 @@
             t_ref[pl.ds(k * LATS * SLOT_ROWS + r, LATS, stride=SLOT_ROWS), :] = zero
 
     def finish(waves, units):
-        high = waves.astype(BF16)
-        low = (waves - high.astype(F32)).astype(BF16)
-        total = dot_nn(high, ones) + dot_nn(low, ones)
-        anomaly = waves - total * (1.0 / members)
+        tiles = [waves[:, t * 128 : (t + 1) * 128] for t in range(3)]
+        lane = lax.broadcasted_iota(jnp.int32, tiles[1].shape, 1)
+        zeros = jnp.zeros_like(tiles[1])
+        folded = jnp.concatenate(
+            [tiles[0] + jnp.where(lane < 64, tiles[1], zeros), tiles[2] + jnp.where(lane < 64, zeros, tiles[1])], axis=1
+        )
+        high = folded.astype(BF16)
+        low = (folded - high.astype(F32)).astype(BF16)
+        mean = (dot_nn(high, ones) + dot_nn(low, ones)) * (1.0 / members)
+        middle = jnp.where(lane < 64, mean[:, :128], mean[:, 128:])
+        anomaly = waves - jnp.concatenate([mean[:, :128], middle, mean[:, 128:]], axis=1)
         for u, (i, j) in enumerate(units):
             for t, (k, r) in enumerate(place(i, j)):
                 t_ref[pl.ds(k * LATS * SLOT_ROWS + r, LATS, stride=SLOT_ROWS), :] = anomaly[

time: 114 us -> 113 us (level)
  Pallas kernels: 14 us -> 12.8 us
where the time goes in v6:
time: 113 us
  blocking collectives  100 us (88%)
  Pallas kernels  12.8 us (11%)
    all_to_all x4, blocking collectives, exchange(): return lax.all_to_all(x, axis, split_axis=0, concat_axis=0, tiled=True)  100 us
    pallas_call x1, Pallas kernels, fourier(): pl.pallas_call(functools.partial(fourier_kernel, members, lev_rows, lat_r...  7.03 us

profile of v6, /device:TPU:1, one launch (start us, length us, event | category | flops | bytes accessed | tf_op | source)
XLA Modules:
  0.0 112.9 jit_solution(9644806193370426277)
XLA Ops:
  0.0 7.0 %fourier.1 = bf16[2816,384]{1,0:T(8,128)(2,1)S(1)} custom-call(f32[12,128,1024]{2,1,0:T(8,128)} %bitcast.7, bf16[8,256,256]{2,1,0:T(8,128)(2,1)} %leg_hbm.1, bf16[256,256]{1,0:T(8,128)(2,1)} %constant.6.clone.refs_0_, bf16[256,256]{1,0:T(8,128)(2,1)} %constant.7.clone.refs_1_, bf16[512,512]{1,0:T(8,128)(2,1)} %constant.8.clone.refs_2_), custom_call_target="tpu_custom_call" | custom-call | flops 5000000000 | bytes 10000000 | tf_op jit(solution)/shard_map/fourier/pallas_call | solution.py:161
  7.0 38.0 %all_to_all.20.r_ref = bf16[32,88,384]{2,1,0:T(8,128)(2,1)S(1)} all-to-all(bf16[32,88,384]{2,1,0:T(8,128)(2,1)S(1)} %bitcast.4), channel_id=1, replica_groups=mesh['lat'=32,'lev'=8] {'lat'}, dimensions={0} | all-to-all | bytes 4325376 | tf_op jit(solution)/shard_map/all_to_all | solution.py:368
  45.0 1.9 %legendre.1 = bf16[3584,128]{1,0:T(8,128)(2,1)S(1)} custom-call(bf16[32,88,384]{2,1,0:T(8,128)(2,1)S(1)} %all_to_all.20.r_ref), custom_call_target="tpu_custom_call" | custom-call | flops 2000000000 | bytes 4000000 | tf_op jit(solution)/shard_map/legendre/pallas_call | solution.py:255
  46.9 38.4 %all_to_all.21 = bf16[256,7,2,128]{3,2,1,0:T(2,128)(2,1)S(1)} all-to-all(bf16[256,7,2,128]{3,2,1,0:T(2,128)(2,1)S(1)} %bitcast.5), channel_id=1, replica_groups=mesh['lat'=32,'lev'=8] {'lev','lat'}, dimensions={0} | all-to-all | bytes 1835008 | tf_op jit(solution)/shard_map/all_to_all | solution.py:368
  85.3 0.0 copy-start
  85.3 1.8 %covariance.1 = bf16[8,32,128]{2,1,0:T(8,128)(2,1)S(1)} custom-call(bf16[3584,128]{1,0:T(8,128)(2,1)S(1)} %bitcast.6), custom_call_target="tpu_custom_call" | custom-call | flops 1000000000 | bytes 2000000 | tf_op jit(solution)/shard_map/covariance/pallas_call | solution.py:308
  87.1 11.1 %all_to_all.22.g_ref = bf16[8,32,128]{2,1,0:T(8,128)(2,1)S(1)} all-to-all(bf16[8,32,128]{2,1,0:T(8,128)(2,1)S(1)} %covariance.1), channel_id=1, replica_groups=mesh['lat'=32,'lev'=8] {'lev'}, dimensions={0} | all-to-all | bytes 131072 | tf_op jit(solution)/shard_map/all_to_all | solution.py:368
  98.1 0.0 copy-done
  98.1 0.9 route.1
  99.0 12.5 %all_to_all.23.r_ref = bf16[32,16,128]{2,1,0:T(8,128)(2,1)S(1)} all-to-all(bf16[32,16,128]{2,1,0:T(8,128)(2,1)S(1)} %route.1), channel_id=1, replica_groups=mesh['lat'=32,'lev'=8] {'lat'}, dimensions={0} | all-to-all | bytes 262144 | tf_op jit(solution)/shard_map/all_to_all | solution.py:368
  111.6 1.3 %collect.1 = f32[16,16,128]{2,1,0:T(8,128)} custom-call(s32[32]{0:T(128)S(1)} %copy-done, bf16[32,16,128]{2,1,0:T(8,128)(2,1)S(1)} %all_to_all.23.r_ref), custom_call_target="tpu_custom_call" | custom-call | tf_op jit(solution)/shard_map/collect/pallas_call | solution.py:357
Async XLA Ops:
  85.3 12.9 %copy-start = (s32[32]{0:T(128)S(1)}, s32[32]{0:T(128)}, u32[]{:S(2)}) copy-start(s32[32]{0:T(128)} %counts_ref.3) | copy-start | bytes 388

commit v7 on v6

--- a/solution.py
+++ b/solution.py
@@ -46,11 +46,11 @@
     return lax.dot_general(a, b, (((1,), (0,)), ((), ())), preferred_element_type=F32)
 
 
-def fourier_kernel(members, lev_rows, lat_rows, f_hbm, leg_hbm, *refs):
+def fourier_kernel(members, lev_rows, lat_rows, f_hbm, *refs):
     classes = len(CLASSES)
-    tab_hbm, (out_ref, f_ref, leg_ref), refs = refs[:classes], refs[classes : classes + 3], refs[classes + 3 :]
+    tab_hbm, (out_ref, f_ref), refs = refs[:classes], refs[classes : classes + 2], refs[classes + 2 :]
     tab_refs, high_refs, low_refs = refs[:classes], refs[classes : 2 * classes], refs[2 * classes : 3 * classes]
-    t_ref, f_sem, sem = refs[3 * classes :]
+    f_sem, sem = refs[3 * classes :]
     pieces = f_ref.shape[0]
     block_rows = lev_rows * lat_rows
 
@@ -59,31 +59,12 @@
         source = f_hbm.at[b, :, piece * 128 : (piece + 1) * 128]
         return pltpu.make_async_copy(source, f_ref.at[piece, rows, :], f_sem.at[b, piece])
 
-    leg_copy = pltpu.make_async_copy(leg_hbm, leg_ref, sem.at[classes])
     tab_copies = [pltpu.make_async_copy(tab_hbm[c], tab_refs[c], sem.at[c]) for c in range(classes)]
     for b in range(members):
         for piece in range(pieces):
             fetch(b, piece).start()
     for copy in tab_copies:
         copy.start()
-    leg_copy.start()
-
-    def pack(lat):
-        table = leg_ref[lat].astype(F32)
-        lane = lax.broadcasted_iota(jnp.int32, (STRIDE, 2 * 128), 1)
-
-        def block(i):
-            return table[STRIDE * i : STRIDE * (i + 1), :]
-
-        tiles = [block(0)[:, :128], block(0)[:, 128:]]
-        for p in range(1, BLOCKS // 2):
-            other = pltpu.roll(block(BLOCKS - p), STRIDE * p, 1)
-            packed = jnp.where(lane >= STRIDE * p, block(p), other)
-            tiles += [packed[:, :128], packed[:, 128:]]
-        tiles.append(block(BLOCKS // 2)[:, 128:])
-        for t, tile in enumerate(tiles):
-            first = (t // 3) * lat_rows
-            t_ref[t % 3, pl.ds(first + lat, LATS, stride=LEG_ROWS), :] = tile
 
     group = lat_rows // 2
     main = 128 // lev_rows
@@ -118,13 +99,9 @@
     lax.fori_loop(0, members, split, 0)
     for copy in tab_copies:
         copy.wait()
-    leg_copy.wait()
-    waiting = list(range(lat_rows))
     for g in range(2):
         columns = slice(g * width, (g + 1) * width)
         for c, (first, step, fold) in enumerate(CLASSES):
-            for k in range(2 if fold == 2 else 1):
-                pack(waiting.pop())
             tab, h, l = tab_refs[c][...], high_refs[c][columns], low_refs[c][columns]
             double = tab.shape[0] // 2
             products = dot_nt(tab, h)
@@ -143,35 +120,68 @@
                 for t, tile in enumerate((acc[:count, here], middle, acc[count:, here])):
                     tile = tile.astype(BF16)
                     for n in range(count // BLOCKS):
-                        start = (first + step * n) * ROWS + (g * group + k) * BLOCKS
+                        start = (first + step * n) * SPEC_ROWS + (g * group + k) * BLOCKS
                         out_ref[start : start + BLOCKS, t * 128 : (t + 1) * 128] = tile[n * BLOCKS : (n + 1) * BLOCKS]
+
+
+def pack_kernel(lat_rows, leg_ref, out_ref, t_ref):
+    def pack(lat):
+        table = leg_ref[lat].astype(F32)
+        lane = lax.broadcasted_iota(jnp.int32, (STRIDE, 2 * 128), 1)
+
+        def block(i):
+            return table[STRIDE * i : STRIDE * (i + 1), :]
+
+        tiles = [block(0)[:, :128], block(0)[:, 128:]]
+        for p in range(1, BLOCKS // 2):
+            other = pltpu.roll(block(BLOCKS - p), STRIDE * p, 1)
+            packed = jnp.where(lane >= STRIDE * p, block(p), other)
+            tiles += [packed[:, :128], packed[:, 128:]]
+        tiles.append(block(BLOCKS // 2)[:, 128:])
+        for t, tile in enumerate(tiles):
+            first = (t // 3) * lat_rows
+            t_ref[t % 3, pl.ds(first + lat, LATS, stride=LEG_ROWS), :] = tile
+
+    for lat in range(lat_rows):
+        pack(lat)
     for t in range(3):
         for d in range(LATS):
             packed = t_ref[t, d * LEG_ROWS : (d + 1) * LEG_ROWS, :]
-            out_ref[d * ROWS + SPEC_ROWS : (d + 1) * ROWS, t * 128 : (t + 1) * 128] = packed.astype(BF16)
-
-
-def fourier(fields, legendre):
+            out_ref[d * LEG_ROWS : (d + 1) * LEG_ROWS, t * 128 : (t + 1) * 128] = packed.astype(BF16)
+
+
+def pack_stage(legendre):
+    return pl.pallas_call(
+        functools.partial(pack_kernel, legendre.shape[0]),
+        in_specs=[pl.BlockSpec(memory_space=VMEM)],
+        out_specs=pl.BlockSpec(memory_space=VMEM),
+        out_shape=jax.ShapeDtypeStruct((LATS * LEG_ROWS, 3 * 128), BF16),
+        scratch_shapes=[VMEM((3, LATS * LEG_ROWS, 128), F32)],
+        compiler_params=pltpu.CompilerParams(vmem_limit_bytes=40 << 20),
+        cost_estimate=pl.CostEstimate(flops=10**8, bytes_accessed=2 * 10**6, transcendentals=0),
+        name="pack",
+    )(legendre)
+
+
+def fourier(fields):
     members, lev_rows, lat_rows, points = fields.shape
-    modes = legendre.shape[1]
+    modes = LATS * BLOCKS
     columns, pieces = 2 * members * lev_rows, points // 128
     tables = fourier_tables(points, modes)
     splits = [VMEM((lat_rows * members * lev_rows, table.shape[1]), BF16) for table in tables]
-    operands = [fields.reshape(members, lev_rows * lat_rows, points), legendre] + [jnp.asarray(t) for t in tables]
+    operands = [fields.reshape(members, lev_rows * lat_rows, points)] + [jnp.asarray(t) for t in tables]
     return pl.pallas_call(
         functools.partial(fourier_kernel, members, lev_rows, lat_rows),
         in_specs=[pl.BlockSpec(memory_space=pltpu.HBM)] * len(operands),
         out_specs=pl.BlockSpec(memory_space=VMEM),
-        out_shape=jax.ShapeDtypeStruct((LATS * ROWS, columns), BF16),
+        out_shape=jax.ShapeDtypeStruct((LATS * SPEC_ROWS, columns), BF16),
         scratch_shapes=[
             VMEM((pieces, members * lev_rows * lat_rows, 128), F32),
-            VMEM(legendre.shape, BF16),
             *[VMEM(table.shape, BF16) for table in tables],
             *splits,
             *splits,
-            VMEM((3, LATS * LEG_ROWS, 128), F32),
             pltpu.SemaphoreType.DMA((members, pieces)),
-            pltpu.SemaphoreType.DMA((len(tables) + 1,)),
+            pltpu.SemaphoreType.DMA((len(tables),)),
         ],
         compiler_params=pltpu.CompilerParams(vmem_limit_bytes=40 << 20),
         cost_estimate=pl.CostEstimate(flops=5 * 10**9, bytes_accessed=10**7, transcendentals=0),
@@ -185,20 +195,20 @@
     return [(2 * p + (base + t) // USED_ROWS, (base + t) % USED_ROWS) for t in range(3)]
 
 
-def legendre_kernel(members, lev_rows, lat_rows, r_ref, out_ref, t_ref, s_ref):
+def legendre_kernel(members, lev_rows, lat_rows, r_ref, leg_ref, out_ref, t_ref, s_ref):
     columns = r_ref.shape[2]
     lats = LATS * lat_rows
     for t in range(3):
         for s in range(LATS):
             rows = slice(s * SPEC_ROWS, (s + 1) * SPEC_ROWS)
-            s_ref[t, rows, :] = r_ref[s, :SPEC_ROWS, t * 128 : (t + 1) * 128].astype(F32)
+            s_ref[t, rows, :] = r_ref[s, :, t * 128 : (t + 1) * 128].astype(F32)
 
     def rows_of(first, lanes):
-        x = r_ref[:, first : first + lat_rows, lanes].astype(F32)
+        x = leg_ref[:, first : first + lat_rows, lanes].astype(F32)
         return x.reshape(lats, -1).astype(BF16)
 
     def table(t):
-        return rows_of(SPEC_ROWS + (t // 3) * lat_rows, slice((t % 3) * 128, (t % 3 + 1) * 128))
+        return rows_of((t // 3) * lat_rows, slice((t % 3) * 128, (t % 3 + 1) * 128))
 
     def spectra(i):
         tiles = [s_ref[t, pl.ds(i, lats, stride=BLOCKS), :] for t in range(3)]
@@ -250,18 +260,18 @@
         out_ref[k * step : (k + 1) * step, :] = t_ref[k * step : (k + 1) * step, :].astype(BF16)
 
 
-def legendre_stage(received, members, lev_rows, lat_rows):
+def legendre_stage(received, table, members, lev_rows, lat_rows):
     rows = LATS * LEVS * SLOT_ROWS
     return pl.pallas_call(
         functools.partial(legendre_kernel, members, lev_rows, lat_rows),
-        in_specs=[pl.BlockSpec(memory_space=VMEM)],
+        in_specs=[pl.BlockSpec(memory_space=VMEM)] * 2,
         out_specs=pl.BlockSpec(memory_space=VMEM),
         out_shape=jax.ShapeDtypeStruct((rows, 128), BF16),
         scratch_shapes=[VMEM((rows, 128), F32), VMEM((3, LATS * SPEC_ROWS, 128), F32)],
         compiler_params=pltpu.CompilerParams(vmem_limit_bytes=40 << 20),
         cost_estimate=pl.CostEstimate(flops=2 * 10**9, bytes_accessed=4 * 10**6, transcendentals=0),
         name="legendre",
-    )(received)
+    )(received, table)
 
 
 def home(lev):
@@ -372,9 +382,9 @@
     members, lev_rows, lat_rows, _ = fields.shape
     modes = legendre.shape[1]
     capacity = 2 * modes // owner_counts.shape[0]
-    first = fourier(fields, legendre)
-    first = exchange(first.reshape(LATS, ROWS, -1), "lat")
-    second = legendre_stage(first, members, lev_rows, lat_rows)
+    table = exchange(pack_stage(legendre).reshape(LATS, LEG_ROWS, -1), "lat")
+    first = exchange(fourier(fields).reshape(LATS, SPEC_ROWS, -1), "lat")
+    second = legendre_stage(first, table, members, lev_rows, lat_rows)
     second = exchange(second.reshape(LATS * LEVS, SLOT_ROWS // 2, 2, 128), ("lev", "lat"))
     third = covariance_stage(second.reshape(-1, 128), members, lev_rows)
     third = exchange(third, "lev")

time: 113 us -> 118 us (1.044)
  blocking collectives: 100 us -> 88.4 us
  starting transfers between devices: 0 us -> 8.58 us
  waiting for transfers between devices: 0 us -> 5.67 us
  local copies, waits for them, and re-layouts: 0.01 us -> 1.23 us
    all_to_all x4, blocking collectives: 100 us -> 88.4 us  [exchange(): return lax.all_to_all(x, axis, split_axis=0, concat_axis=0, tiled=True)]
    all_to_all x0 -> x1, starting transfers between devices: none -> 8.58 us  [exchange(): return lax.all_to_all(x, axis, split_axis=0, concat_axis=0, tiled=True)]
    all_to_all x0 -> x1, waiting for transfers between devices: none -> 5.67 us  [exchange(): return lax.all_to_all(x, axis, split_axis=0, concat_axis=0, tiled=True)]
    unnamed x2 -> x4, local copies, waits for them, and re-layouts: 0.01 us -> 1.23 us
    pallas_call x0 -> x1, Pallas kernels: none -> 1.18 us  [pack_stage(): pl.pallas_call(functools.partial(pack_kernel, legendre.shape[0]), in_spec...]
  transfers between devices with their start and end apart: 0 -> 1, of which waited for: 0 -> 1; matrix products, arithmetic and copies ran while one was open for 0% -> 0% of each run, Pallas kernels for 0% -> 6%
where the time goes in v7:
time: 118 us; the launch traced here: 117 us
  blocking collectives  88.4 us (75%)
  Pallas kernels  13.4 us (11%)
  starting transfers between devices  8.58 us (7%)
  waiting for transfers between devices  5.67 us (5%)
  local copies, waits for them, and re-layouts  1.23 us (1%)
    all_to_all x4, blocking collectives, exchange(): return lax.all_to_all(x, axis, split_axis=0, concat_axis=0, tiled=True)  88.4 us
    all_to_all x1, starting transfers between devices, exchange(): return lax.all_to_all(x, axis, split_axis=0, concat_axis=0, tiled=True)  8.58 us
    pallas_call x1, Pallas kernels, fourier(): pl.pallas_call(functools.partial(fourier_kernel, members, lev_rows, lat_r...  6.46 us
    all_to_all x1, waiting for transfers between devices, exchange(): return lax.all_to_all(x, axis, split_axis=0, concat_axis=0, tiled=True)  5.67 us
  transfers between devices with their start and end apart: 1, of which 1 were waited for; matrix products, arithmetic and copies ran while one was open for 0% of the time, Pallas kernels for 6%

profile of v7, /device:TPU:1, one launch (start us, length us, event | category | flops | bytes accessed | tf_op | source)
XLA Modules:
  0.0 117.3 jit_solution(15667027579405248878)
XLA Ops:
  0.0 0.0 copy-start
  0.0 1.2 %copy-done = bf16[8,256,256]{2,1,0:T(8,128)(2,1)S(1)} copy-done((bf16[8,256,256]{2,1,0:T(8,128)(2,1)S(1)}, bf16[8,256,256]{2,1,0:T(8,128)(2,1)}, u32[]{:S(2)}) %copy-start) | copy-done | bytes 1048600
  1.2 1.2 %pack.1 = bf16[768,384]{1,0:T(8,128)(2,1)} custom-call(bf16[8,256,256]{2,1,0:T(8,128)(2,1)S(1)} %copy-done), custom_call_target="tpu_custom_call" | custom-call | flops 100000000 | bytes 2000000 | tf_op jit(solution)/shard_map/pack/pallas_call | solution.py:154
  2.4 8.6 %all-to-all-start.1 = ((bf16[32,24,384]{2,1,0:T(8,128)(2,1)}), bf16[32,24,384]{2,1,0:T(8,128)(2,1)S(1)}, u32[]{:S(2)}, u32[]{:S(2)}) async-start(bf16[32,24,384]{2,1,0:T(8,128)(2,1)} %bitcast.2), calls=%async_computation.1 | async-start | bytes 1179648 | tf_op jit(solution)/shard_map/all_to_all | solution.py:378
  11.0 6.5 %fourier.1 = bf16[2048,384]{1,0:T(8,128)(2,1)S(1)} custom-call(f32[12,128,1024]{2,1,0:T(8,128)} %bitcast.8, bf16[256,256]{1,0:T(8,128)(2,1)} %constant.6.clone.refs_0_, bf16[256,256]{1,0:T(8,128)(2,1)} %constant.7.clone.refs_1_, bf16[512,512]{1,0:T(8,128)(2,1)} %constant.8.clone.refs_2_), custom_call_target="tpu_custom_call" | custom-call | flops 5000000000 | bytes 10000000 | tf_op jit(solution)/shard_map/fourier/pallas_call | solution.py:173
  17.5 5.7 %all-to-all-done.1.leg_ref = bf16[32,24,384]{2,1,0:T(8,128)(2,1)S(1)} async-done(((bf16[32,24,384]{2,1,0:T(8,128)(2,1)}), bf16[32,24,384]{2,1,0:T(8,128)(2,1)S(1)}, u32[]{:S(2)}, u32[]{:S(2)}) %all-to-all-start.1) | async-done | bytes 589856 | tf_op jit(solution)/shard_map/all_to_all | solution.py:378
  23.1 26.3 %all_to_all.25.r_ref = bf16[32,64,384]{2,1,0:T(8,128)(2,1)S(1)} all-to-all(bf16[32,64,384]{2,1,0:T(8,128)(2,1)S(1)} %bitcast.5), channel_id=1, replica_groups=mesh['lat'=32,'lev'=8] {'lat'}, dimensions={0} | all-to-all | bytes 3145728 | tf_op jit(solution)/shard_map/all_to_all | solution.py:378
  49.4 1.9 %legendre.1 = bf16[3584,128]{1,0:T(8,128)(2,1)S(1)} custom-call(bf16[32,64,384]{2,1,0:T(8,128)(2,1)S(1)} %all_to_all.25.r_ref, bf16[32,24,384]{2,1,0:T(8,128)(2,1)S(1)} %all-to-all-done.1.leg_ref), custom_call_target="tpu_custom_call" | custom-call | flops 2000000000 | bytes 4000000 | tf_op jit(solution)/shard_map/legendre/pallas_call | solution.py:265
  51.3 38.5 %all_to_all.26 = bf16[256,7,2,128]{3,2,1,0:T(2,128)(2,1)S(1)} all-to-all(bf16[256,7,2,128]{3,2,1,0:T(2,128)(2,1)S(1)} %bitcast.6), channel_id=1, replica_groups=mesh['lat'=32,'lev'=8] {'lev','lat'}, dimensions={0} | all-to-all | bytes 1835008 | tf_op jit(solution)/shard_map/all_to_all | solution.py:378
  89.7 0.0 copy-start.1
  89.8 1.8 %covariance.1 = bf16[8,32,128]{2,1,0:T(8,128)(2,1)S(1)} custom-call(bf16[3584,128]{1,0:T(8,128)(2,1)S(1)} %bitcast.7), custom_call_target="tpu_custom_call" | custom-call | flops 1000000000 | bytes 2000000 | tf_op jit(solution)/shard_map/covariance/pallas_call | solution.py:318
  91.6 11.1 %all_to_all.27.g_ref = bf16[8,32,128]{2,1,0:T(8,128)(2,1)S(1)} all-to-all(bf16[8,32,128]{2,1,0:T(8,128)(2,1)S(1)} %covariance.1), channel_id=1, replica_groups=mesh['lat'=32,'lev'=8] {'lev'}, dimensions={0} | all-to-all | bytes 131072 | tf_op jit(solution)/shard_map/all_to_all | solution.py:378
  102.6 0.0 copy-done.1
  102.6 0.9 route.1
  103.5 12.5 %all_to_all.28.r_ref = bf16[32,16,128]{2,1,0:T(8,128)(2,1)S(1)} all-to-all(bf16[32,16,128]{2,1,0:T(8,128)(2,1)S(1)} %route.1), channel_id=1, replica_groups=mesh['lat'=32,'lev'=8] {'lat'}, dimensions={0} | all-to-all | bytes 262144 | tf_op jit(solution)/shard_map/all_to_all | solution.py:378
  116.0 1.3 %collect.1 = f32[16,16,128]{2,1,0:T(8,128)} custom-call(s32[32]{0:T(128)S(1)} %copy-done.1, bf16[32,16,128]{2,1,0:T(8,128)(2,1)S(1)} %all_to_all.28.r_ref), custom_call_target="tpu_custom_call" | custom-call | tf_op jit(solution)/shard_map/collect/pallas_call | solution.py:367
Async XLA Ops:
  0.0 1.2 %copy-start = (bf16[8,256,256]{2,1,0:T(8,128)(2,1)S(1)}, bf16[8,256,256]{2,1,0:T(8,128)(2,1)}, u32[]{:S(2)}) copy-start(bf16[8,256,256]{2,1,0:T(8,128)(2,1)} %leg_ref.1) | copy-start | bytes 3145732
  2.4 20.7 %all-to-all-start.1 = ((bf16[32,24,384]{2,1,0:T(8,128)(2,1)}), bf16[32,24,384]{2,1,0:T(8,128)(2,1)S(1)}, u32[]{:S(2)}, u32[]{:S(2)}) async-start(bf16[32,24,384]{2,1,0:T(8,128)(2,1)} %bitcast.2), calls=%async_computation.1 | async-start | bytes 1179648 | tf_op jit(solution)/shard_map/all_to_all | solution.py:378
  89.7 12.9 %copy-start.1 = (s32[32]{0:T(128)S(1)}, s32[32]{0:T(128)}, u32[]{:S(2)}) copy-start(s32[32]{0:T(128)} %counts_ref.3) | copy-start | bytes 388

commit v8 on v6

--- a/solution.py
+++ b/solution.py
@@ -51,19 +51,18 @@
     tab_hbm, (out_ref, f_ref, leg_ref), refs = refs[:classes], refs[classes : classes + 3], refs[classes + 3 :]
     tab_refs, high_refs, low_refs = refs[:classes], refs[classes : 2 * classes], refs[2 * classes : 3 * classes]
     t_ref, f_sem, sem = refs[3 * classes :]
-    pieces = f_ref.shape[0]
-    block_rows = lev_rows * lat_rows
-
-    def fetch(b, piece):
-        rows = pl.ds(pl.multiple_of(b * block_rows, block_rows), block_rows)
-        source = f_hbm.at[b, :, piece * 128 : (piece + 1) * 128]
-        return pltpu.make_async_copy(source, f_ref.at[piece, rows, :], f_sem.at[b, piece])
+    unit, pitch = f_hbm.shape[1], f_ref.shape[1]
+    pieces = unit // lat_rows
+    flat = f_ref.reshape(f_ref.shape[0] * pitch, 128)
+
+    def fetch(b):
+        rows = pl.ds(b * lev_rows, lev_rows)
+        return pltpu.make_async_copy(f_hbm.at[rows], f_ref.at[rows, pl.ds(0, unit), :], f_sem.at[b])
 
     leg_copy = pltpu.make_async_copy(leg_hbm, leg_ref, sem.at[classes])
     tab_copies = [pltpu.make_async_copy(tab_hbm[c], tab_refs[c], sem.at[c]) for c in range(classes)]
     for b in range(members):
-        for piece in range(pieces):
-            fetch(b, piece).start()
+        fetch(b).start()
     for copy in tab_copies:
         copy.start()
     leg_copy.start()
@@ -91,10 +90,8 @@
     width = group * members * lev_rows
 
     def split(b, carry):
-        for piece in range(pieces):
-            fetch(b, piece).wait()
+        fetch(b).wait()
         for lat in range(lat_rows):
-            every = pl.ds(b * block_rows + lat, lev_rows, stride=lat_rows)
             k = lat % group
             inside = jnp.where(b < main, k * 128 + b * lev_rows, group * 128 + (k * rest + b - main) * lev_rows)
             rows = pl.ds(pl.multiple_of(lat // group * width + inside, lev_rows), lev_rows)
@@ -107,7 +104,10 @@
 
             quarter = pieces // 4
             for piece in range(quarter):
-                x0, x1, x2, x3 = [f_ref[piece + q * quarter, every, :] for q in range(4)]
+                x0, x1, x2, x3 = [
+                    flat[pl.ds((b * lev_rows) * pitch + (piece + q * quarter) * lat_rows + lat, lev_rows, stride=pitch), :]
+                    for q in range(4)
+                ]
                 even, odd = x0 + x2, x1 + x3
                 store(0, piece, even + odd)
                 store(1, piece, even - odd)
@@ -157,20 +157,21 @@
     columns, pieces = 2 * members * lev_rows, points // 128
     tables = fourier_tables(points, modes)
     splits = [VMEM((lat_rows * members * lev_rows, table.shape[1]), BF16) for table in tables]
-    operands = [fields.reshape(members, lev_rows * lat_rows, points), legendre] + [jnp.asarray(t) for t in tables]
+    rows = fields.reshape(members, lev_rows, lat_rows, pieces, 128).swapaxes(2, 3).reshape(members * lev_rows, pieces * lat_rows, 128)
+    operands = [rows, legendre] + [jnp.asarray(t) for t in tables]
     return pl.pallas_call(
         functools.partial(fourier_kernel, members, lev_rows, lat_rows),
         in_specs=[pl.BlockSpec(memory_space=pltpu.HBM)] * len(operands),
         out_specs=pl.BlockSpec(memory_space=VMEM),
         out_shape=jax.ShapeDtypeStruct((LATS * ROWS, columns), BF16),
         scratch_shapes=[
-            VMEM((pieces, members * lev_rows * lat_rows, 128), F32),
+            VMEM((members * lev_rows, pieces * lat_rows + 8, 128), F32),
             VMEM(legendre.shape, BF16),
             *[VMEM(table.shape, BF16) for table in tables],
             *splits,
             *splits,
             VMEM((3, LATS * LEG_ROWS, 128), F32),
-            pltpu.SemaphoreType.DMA((members, pieces)),
+            pltpu.SemaphoreType.DMA((members,)),
             pltpu.SemaphoreType.DMA((len(tables) + 1,)),
         ],
         compiler_params=pltpu.CompilerParams(vmem_limit_bytes=40 << 20),

time: 113 us -> 112 us (level)
  no operation moved by 1% of the time
where the time goes in v8:
time: 112 us
  blocking collectives  100 us (89%)
  Pallas kernels  11.9 us (11%)
    all_to_all x4, blocking collectives, exchange(): return lax.all_to_all(x, axis, split_axis=0, concat_axis=0, tiled=True)  100 us
    pallas_call x1, Pallas kernels, fourier(): pl.pallas_call(functools.partial(fourier_kernel, members, lev_rows, lat_r...  6.08 us

profile of v8, /device:TPU:1, one launch (start us, length us, event | category | flops | bytes accessed | tf_op | source)
XLA Modules:
  0.0 111.9 jit_solution(17908576400592926588)
XLA Ops:
  0.0 6.1 %fourier.1 = bf16[2816,384]{1,0:T(8,128)(2,1)S(1)} custom-call(f32[192,64,128]{2,1,0:T(8,128)} %bitcast.11, bf16[8,256,256]{2,1,0:T(8,128)(2,1)} %leg_hbm.1, bf16[256,256]{1,0:T(8,128)(2,1)} %constant.6.clone.refs_0_, bf16[256,256]{1,0:T(8,128)(2,1)} %constant.7.clone.refs_1_, bf16[512,512]{1,0:T(8,128)(2,1)} %constant.8.clone.refs_2_), custom_call_target="tpu_custom_call" | custom-call | flops 5000000000 | bytes 10000000 | tf_op jit(solution)/shard_map/fourier/pallas_call | solution.py:162
  6.1 38.0 %all_to_all.20.r_ref = bf16[32,88,384]{2,1,0:T(8,128)(2,1)S(1)} all-to-all(bf16[32,88,384]{2,1,0:T(8,128)(2,1)S(1)} %bitcast.8), channel_id=1, replica_groups=mesh['lat'=32,'lev'=8] {'lat'}, dimensions={0} | all-to-all | bytes 4325376 | tf_op jit(solution)/shard_map/all_to_all | solution.py:369
  44.0 1.9 %legendre.1 = bf16[3584,128]{1,0:T(8,128)(2,1)S(1)} custom-call(bf16[32,88,384]{2,1,0:T(8,128)(2,1)S(1)} %all_to_all.20.r_ref), custom_call_target="tpu_custom_call" | custom-call | flops 2000000000 | bytes 4000000 | tf_op jit(solution)/shard_map/legendre/pallas_call | solution.py:256
  45.9 38.4 %all_to_all.21 = bf16[256,7,2,128]{3,2,1,0:T(2,128)(2,1)S(1)} all-to-all(bf16[256,7,2,128]{3,2,1,0:T(2,128)(2,1)S(1)} %bitcast.9), channel_id=1, replica_groups=mesh['lat'=32,'lev'=8] {'lev','lat'}, dimensions={0} | all-to-all | bytes 1835008 | tf_op jit(solution)/shard_map/all_to_all | solution.py:369
  84.3 0.0 copy-start
  84.3 1.8 %covariance.1 = bf16[8,32,128]{2,1,0:T(8,128)(2,1)S(1)} custom-call(bf16[3584,128]{1,0:T(8,128)(2,1)S(1)} %bitcast.10), custom_call_target="tpu_custom_call" | custom-call | flops 1000000000 | bytes 2000000 | tf_op jit(solution)/shard_map/covariance/pallas_call | solution.py:309
  86.2 11.1 %all_to_all.22.g_ref = bf16[8,32,128]{2,1,0:T(8,128)(2,1)S(1)} all-to-all(bf16[8,32,128]{2,1,0:T(8,128)(2,1)S(1)} %covariance.1), channel_id=1, replica_groups=mesh['lat'=32,'lev'=8] {'lev'}, dimensions={0} | all-to-all | bytes 131072 | tf_op jit(solution)/shard_map/all_to_all | solution.py:369
  97.2 0.0 copy-done
  97.2 0.9 route.1
  98.1 12.5 %all_to_all.23.r_ref = bf16[32,16,128]{2,1,0:T(8,128)(2,1)S(1)} all-to-all(bf16[32,16,128]{2,1,0:T(8,128)(2,1)S(1)} %route.1), channel_id=1, replica_groups=mesh['lat'=32,'lev'=8] {'lat'}, dimensions={0} | all-to-all | bytes 262144 | tf_op jit(solution)/shard_map/all_to_all | solution.py:369
  110.6 1.3 %collect.1 = f32[16,16,128]{2,1,0:T(8,128)} custom-call(s32[32]{0:T(128)S(1)} %copy-done, bf16[32,16,128]{2,1,0:T(8,128)(2,1)S(1)} %all_to_all.23.r_ref), custom_call_target="tpu_custom_call" | custom-call | tf_op jit(solution)/shard_map/collect/pallas_call | solution.py:358
Async XLA Ops:
  84.3 12.9 %copy-start = (s32[32]{0:T(128)S(1)}, s32[32]{0:T(128)}, u32[]{:S(2)}) copy-start(s32[32]{0:T(128)} %counts_ref.3) | copy-start | bytes 388

commit v9 on v8

--- a/solution.py
+++ b/solution.py
@@ -275,29 +275,17 @@
     count = LATS * SLOT_ROWS
     lev, lat = lax.axis_index("lev"), lax.axis_index("lat")
     p, h = home(lev)
-    parts = [y_ref[v * count : (v + 1) * count, :] for v in range(LEVS)]
-    lane = lax.broadcasted_iota(jnp.int32, (count, 128), 1)
-    for bit in (1, 2, 4):
-        shift = bit * lev_rows
-        low = (lane // shift) % 2 == 0
-        swapped = list(parts)
-        for v in range(LEVS):
-            if v & bit:
-                continue
-            a, b = parts[v], parts[v | bit]
-            swapped[v] = jnp.where(low, a, pltpu.roll(b, shift, 1))
-            swapped[v | bit] = jnp.where(low, pltpu.roll(a, 128 - shift, 1), b)
-        parts = swapped
+    turned = [y_ref[v * count : (v + 1) * count, :].T for v in range(LEVS)]
     first_rows = jnp.where(h == 0, 3 * (p + 1), 0)
     slot = lax.broadcasted_iota(jnp.int32, (levels, count), 1) % SLOT_ROWS
     is_first = slot < first_rows
+    zero = jnp.zeros((levels, count), BF16)
     one = jnp.zeros((levels, levels), F32)
     two = jnp.zeros((levels, levels), F32)
-    for part in parts:
-        turned = part.astype(F32).T
-        zero = jnp.zeros_like(turned)
-        one += dot_nn(jnp.where(is_first, turned, zero).astype(BF16), part)
-        two += dot_nn(jnp.where(is_first, zero, turned).astype(BF16), part)
+    for b in range(128 // lev_rows):
+        part = jnp.concatenate([t[b * lev_rows : (b + 1) * lev_rows] for t in turned], axis=0)
+        one += dot_nt(jnp.where(is_first, part, zero), part)
+        two += dot_nt(jnp.where(is_first, zero, part), part)
     for s, (total, n) in enumerate(((one, lat + STRIDE * p), (two, lat + STRIDE * (BLOCKS - 1 - p)))):
         divisor = ((members - 1) * (2 * n + 2)).astype(F32)
         scaled = (total / jnp.full((levels, levels), divisor, F32)).astype(BF16)

time: 112 us -> 111 us (level)
  no operation moved by 1% of the time
where the time goes in v9:
time: 111 us
  blocking collectives  100 us (90%)
  Pallas kernels  11.1 us (10%)
    all_to_all x4, blocking collectives, exchange(): return lax.all_to_all(x, axis, split_axis=0, concat_axis=0, tiled=True)  100 us
    pallas_call x1, Pallas kernels, fourier(): pl.pallas_call(functools.partial(fourier_kernel, members, lev_rows, lat_r...  6.08 us

profile of v9, /device:TPU:1, one launch (start us, length us, event | category | flops | bytes accessed | tf_op | source)
XLA Modules:
  0.0 111.1 jit_solution(13433113866042955042)
XLA Ops:
  0.0 6.1 %fourier.1 = bf16[2816,384]{1,0:T(8,128)(2,1)S(1)} custom-call(f32[192,64,128]{2,1,0:T(8,128)} %bitcast.11, bf16[8,256,256]{2,1,0:T(8,128)(2,1)} %leg_hbm.1, bf16[256,256]{1,0:T(8,128)(2,1)} %constant.6.clone.refs_0_, bf16[256,256]{1,0:T(8,128)(2,1)} %constant.7.clone.refs_1_, bf16[512,512]{1,0:T(8,128)(2,1)} %constant.8.clone.refs_2_), custom_call_target="tpu_custom_call" | custom-call | flops 5000000000 | bytes 10000000 | tf_op jit(solution)/shard_map/fourier/pallas_call | solution.py:162
  6.1 38.0 %all_to_all.20.r_ref = bf16[32,88,384]{2,1,0:T(8,128)(2,1)S(1)} all-to-all(bf16[32,88,384]{2,1,0:T(8,128)(2,1)S(1)} %bitcast.8), channel_id=1, replica_groups=mesh['lat'=32,'lev'=8] {'lat'}, dimensions={0} | all-to-all | bytes 4325376 | tf_op jit(solution)/shard_map/all_to_all | solution.py:357
  44.0 1.9 %legendre.1 = bf16[3584,128]{1,0:T(8,128)(2,1)S(1)} custom-call(bf16[32,88,384]{2,1,0:T(8,128)(2,1)S(1)} %all_to_all.20.r_ref), custom_call_target="tpu_custom_call" | custom-call | flops 2000000000 | bytes 4000000 | tf_op jit(solution)/shard_map/legendre/pallas_call | solution.py:256
  45.9 38.4 %all_to_all.21 = bf16[256,7,2,128]{3,2,1,0:T(2,128)(2,1)S(1)} all-to-all(bf16[256,7,2,128]{3,2,1,0:T(2,128)(2,1)S(1)} %bitcast.9), channel_id=1, replica_groups=mesh['lat'=32,'lev'=8] {'lev','lat'}, dimensions={0} | all-to-all | bytes 1835008 | tf_op jit(solution)/shard_map/all_to_all | solution.py:357
  84.3 0.0 copy-start
  84.3 1.0 covariance.1
  85.3 11.1 %all_to_all.22.g_ref = bf16[8,32,128]{2,1,0:T(8,128)(2,1)S(1)} all-to-all(bf16[8,32,128]{2,1,0:T(8,128)(2,1)S(1)} %covariance.1), channel_id=1, replica_groups=mesh['lat'=32,'lev'=8] {'lev'}, dimensions={0} | all-to-all | bytes 131072 | tf_op jit(solution)/shard_map/all_to_all | solution.py:357
  96.4 0.0 copy-done
  96.4 0.9 route.1
  97.3 12.5 %all_to_all.23.r_ref = bf16[32,16,128]{2,1,0:T(8,128)(2,1)S(1)} all-to-all(bf16[32,16,128]{2,1,0:T(8,128)(2,1)S(1)} %route.1), channel_id=1, replica_groups=mesh['lat'=32,'lev'=8] {'lat'}, dimensions={0} | all-to-all | bytes 262144 | tf_op jit(solution)/shard_map/all_to_all | solution.py:357
  109.8 1.3 %collect.1 = f32[16,16,128]{2,1,0:T(8,128)} custom-call(s32[32]{0:T(128)S(1)} %copy-done, bf16[32,16,128]{2,1,0:T(8,128)(2,1)S(1)} %all_to_all.23.r_ref), custom_call_target="tpu_custom_call" | custom-call | tf_op jit(solution)/shard_map/collect/pallas_call | solution.py:346
Async XLA Ops:
  84.3 12.1 %copy-start = (s32[32]{0:T(128)S(1)}, s32[32]{0:T(128)}, u32[]{:S(2)}) copy-start(s32[32]{0:T(128)} %counts_ref.3) | copy-start | bytes 388

commit v10 on v9

--- a/solution.py
+++ b/solution.py
@@ -12,6 +12,8 @@
 
 F32, BF16 = jnp.float32, jnp.bfloat16
 LATS, LEVS = 32, 8
+CHIPS = LATS // 2
+LAT = ("y", "x", "core")
 STRIDE = 32
 BLOCKS = 8
 SPEC_ROWS, LEG_ROWS = 64, 24
@@ -265,6 +267,14 @@
     )(received)
 
 
+def chip_index():
+    return lax.axis_index("y") * (CHIPS // 4) + lax.axis_index("x")
+
+
+def residue():
+    return lax.axis_index("core") * CHIPS + chip_index()
+
+
 def home(lev):
     p, h = lev // 2, lev % 2
     return p, h
@@ -273,7 +283,7 @@
 def covariance_kernel(members, lev_rows, y_ref, out_ref):
     levels = LEVS * lev_rows
     count = LATS * SLOT_ROWS
-    lev, lat = lax.axis_index("lev"), lax.axis_index("lat")
+    lev, lat = lax.axis_index("lev"), residue()
     p, h = home(lev)
     turned = [y_ref[v * count : (v + 1) * count, :].T for v in range(LEVS)]
     first_rows = jnp.where(h == 0, 3 * (p + 1), 0)
@@ -306,7 +316,7 @@
 
 
 def route_kernel(lev_rows, counts_ref, g_ref, out_ref, f_ref):
-    lat = lax.axis_index("lat")
+    lat = residue()
     half = BLOCKS // 2
     for j in range(BLOCKS):
         p, s = min(j, BLOCKS - 1 - j), int(j >= half)
@@ -334,11 +344,13 @@
 
 
 def collect_kernel(counts_ref, r_ref, out_ref):
-    lat = lax.axis_index("lat")
+    chip, core = chip_index(), lax.axis_index("core")
+    lat = 2 * chip + core
     start = lax.fori_loop(0, lat, lambda k, s: s + counts_ref[k], jnp.int32(0))
     count = counts_ref[lat]
     for slot in range(out_ref.shape[0]):
-        block = r_ref[(start + slot) % STRIDE].astype(F32)
+        c = (start + slot) % STRIDE
+        block = r_ref[(c % CHIPS) * 2 + c // CHIPS].astype(F32)
         out_ref[slot] = jnp.where(slot < count, block, jnp.zeros_like(block))
 
 
@@ -362,21 +374,22 @@
     modes = legendre.shape[1]
     capacity = 2 * modes // owner_counts.shape[0]
     first = fourier(fields, legendre)
-    first = exchange(first.reshape(LATS, ROWS, -1), "lat")
+    first = exchange(first.reshape(LATS, ROWS, -1), LAT)
     second = legendre_stage(first, members, lev_rows, lat_rows)
-    second = exchange(second.reshape(LATS * LEVS, SLOT_ROWS // 2, 2, 128), ("lev", "lat"))
+    second = exchange(second.reshape(LATS * LEVS, SLOT_ROWS // 2, 2, 128), ("lev", "core", "y", "x"))
     third = covariance_stage(second.reshape(-1, 128), members, lev_rows)
     third = exchange(third, "lev")
     fourth = route_stage(third, owner_counts, lev_rows)
-    fourth = exchange(fourth, "lat")
+    fourth = exchange(fourth, LAT)
     return collect_stage(fourth, owner_counts, capacity, lev_rows)
 
 
 def solution(mesh):
+    parts = jax.sharding.Mesh(mesh.devices.reshape(4, CHIPS // 4, 2, LEVS), (*LAT, "lev"))
     return jax.shard_map(
         on_device,
-        mesh=mesh,
-        in_specs=(P(None, "lev", "lat", None), P("lat", None, None), P()),
-        out_specs=P("lat", "lev", None),
+        mesh=parts,
+        in_specs=(P(None, "lev", LAT, None), P(LAT, None, None), P()),
+        out_specs=P(LAT, "lev", None),
         check_vma=False,
     )

time: 111 us -> 112 us (level)
  no operation moved by 1% of the time
where the time goes in v10:
time: 112 us; the launch traced here: 111 us
  blocking collectives  100 us (89%)
  Pallas kernels  11.2 us (10%)
    all_to_all x4, blocking collectives, exchange(): return lax.all_to_all(x, axis, split_axis=0, concat_axis=0, tiled=True)  100 us
    pallas_call x1, Pallas kernels, fourier(): pl.pallas_call(functools.partial(fourier_kernel, members, lev_rows, lat_r...  6.08 us

profile of v10, /device:TPU:1, one launch (start us, length us, event | category | flops | bytes accessed | tf_op | source)
XLA Modules:
  0.0 111.3 jit_solution(4972241036425384534)
XLA Ops:
  0.0 6.1 %fourier.1 = bf16[2816,384]{1,0:T(8,128)(2,1)S(1)} custom-call(f32[192,64,128]{2,1,0:T(8,128)} %bitcast.11, bf16[8,256,256]{2,1,0:T(8,128)(2,1)} %leg_hbm.1, bf16[256,256]{1,0:T(8,128)(2,1)} %constant.6.clone.refs_0_, bf16[256,256]{1,0:T(8,128)(2,1)} %constant.7.clone.refs_1_, bf16[512,512]{1,0:T(8,128)(2,1)} %constant.8.clone.refs_2_), custom_call_target="tpu_custom_call" | custom-call | flops 5000000000 | bytes 10000000 | tf_op jit(solution)/shard_map/fourier/pallas_call | solution.py:164
  6.1 38.0 %all_to_all.20.r_ref = bf16[32,88,384]{2,1,0:T(8,128)(2,1)S(1)} all-to-all(bf16[32,88,384]{2,1,0:T(8,128)(2,1)S(1)} %bitcast.8), channel_id=1, replica_groups=mesh['y'=4,'x'=4,'core'=2,'lev'=8] {'y','x','core'}, dimensions={0} | all-to-all | bytes 4325376 | tf_op jit(solution)/shard_map/all_to_all | solution.py:369
  44.0 1.9 %legendre.1 = bf16[3584,128]{1,0:T(8,128)(2,1)S(1)} custom-call(bf16[32,88,384]{2,1,0:T(8,128)(2,1)S(1)} %all_to_all.20.r_ref), custom_call_target="tpu_custom_call" | custom-call | flops 2000000000 | bytes 4000000 | tf_op jit(solution)/shard_map/legendre/pallas_call | solution.py:258
  45.9 37.8 %all_to_all.21 = bf16[256,7,2,128]{3,2,1,0:T(2,128)(2,1)S(1)} all-to-all(bf16[256,7,2,128]{3,2,1,0:T(2,128)(2,1)S(1)} %bitcast.9), channel_id=1, replica_groups=mesh['y'=4,'x'=4,'core'=2,'lev'=8] {'lev','core','y','x'}, dimensions={0} | all-to-all | bytes 1835008 | tf_op jit(solution)/shard_map/all_to_all | solution.py:369
  83.7 0.0 copy-start
  83.7 1.0 covariance.1
  84.7 11.5 %all_to_all.22.g_ref = bf16[8,32,128]{2,1,0:T(8,128)(2,1)S(1)} all-to-all(bf16[8,32,128]{2,1,0:T(8,128)(2,1)S(1)} %covariance.1), channel_id=1, replica_groups=mesh['y'=4,'x'=4,'core'=2,'lev'=8] {'lev'}, dimensions={0} | all-to-all | bytes 131072 | tf_op jit(solution)/shard_map/all_to_all | solution.py:369
  96.2 0.0 copy-done
  96.2 0.9 route.1
  97.1 12.8 %all_to_all.23.r_ref = bf16[32,16,128]{2,1,0:T(8,128)(2,1)S(1)} all-to-all(bf16[32,16,128]{2,1,0:T(8,128)(2,1)S(1)} %route.1), channel_id=1, replica_groups=mesh['y'=4,'x'=4,'core'=2,'lev'=8] {'y','x','core'}, dimensions={0} | all-to-all | bytes 262144 | tf_op jit(solution)/shard_map/all_to_all | solution.py:369
  109.9 1.4 %collect.1 = f32[16,16,128]{2,1,0:T(8,128)} custom-call(s32[32]{0:T(128)S(1)} %copy-done, bf16[32,16,128]{2,1,0:T(8,128)(2,1)S(1)} %all_to_all.23.r_ref), custom_call_target="tpu_custom_call" | custom-call | tf_op jit(solution)/shard_map/collect/pallas_call | solution.py:358
Async XLA Ops:
  83.7 12.5 %copy-start = (s32[32]{0:T(128)S(1)}, s32[32]{0:T(128)}, u32[]{:S(2)}) copy-start(s32[32]{0:T(128)} %counts_ref.3) | copy-start | bytes 388

commit v11 on v9

--- a/solution.py
+++ b/solution.py
@@ -313,12 +313,11 @@
         rows = slice(s * lev_rows, (s + 1) * lev_rows)
         f_ref[j] = (g_ref[2 * p, rows, :].astype(F32) + g_ref[2 * p + 1, rows, :].astype(F32)).astype(BF16)
 
-    def step(owner, start):
-        j = jnp.maximum(start - lat + (STRIDE - 1), 0) // STRIDE
+    start = jnp.int32(0)
+    for owner in range(LATS):
+        j = lax.shift_right_logical(start - lat + (STRIDE - 1), 5)
         out_ref[owner] = f_ref[jnp.minimum(j, BLOCKS - 1)]
-        return start + counts_ref[owner]
-
-    lax.fori_loop(0, LATS, step, jnp.int32(0))
+        start += counts_ref[owner]
 
 
 def route_stage(parts, owner_counts, lev_rows):
@@ -335,10 +334,12 @@
 
 def collect_kernel(counts_ref, r_ref, out_ref):
     lat = lax.axis_index("lat")
-    start = lax.fori_loop(0, lat, lambda k, s: s + counts_ref[k], jnp.int32(0))
+    start = jnp.int32(0)
+    for k in range(LATS - 1):
+        start += jnp.where(k < lat, counts_ref[k], 0)
     count = counts_ref[lat]
     for slot in range(out_ref.shape[0]):
-        block = r_ref[(start + slot) % STRIDE].astype(F32)
+        block = r_ref[jnp.bitwise_and(start + slot, STRIDE - 1)].astype(F32)
         out_ref[slot] = jnp.where(slot < count, block, jnp.zeros_like(block))
 
 

time: 111 us -> 111 us (level)
  no operation moved by 1% of the time
where the time goes in v11:
time: 111 us
  blocking collectives  100 us (90%)
  Pallas kernels  10.8 us (10%)
    all_to_all x4, blocking collectives, exchange(): return lax.all_to_all(x, axis, split_axis=0, concat_axis=0, tiled=True)  100 us
    pallas_call x1, Pallas kernels, fourier(): pl.pallas_call(functools.partial(fourier_kernel, members, lev_rows, lat_r...  6.08 us

profile of v11, /device:TPU:1, one launch (start us, length us, event | category | flops | bytes accessed | tf_op | source)
XLA Modules:
  0.0 110.8 jit_solution(11460793104377167456)
XLA Ops:
  0.0 6.1 %fourier.1 = bf16[2816,384]{1,0:T(8,128)(2,1)S(1)} custom-call(f32[192,64,128]{2,1,0:T(8,128)} %bitcast.11, bf16[8,256,256]{2,1,0:T(8,128)(2,1)} %leg_hbm.1, bf16[256,256]{1,0:T(8,128)(2,1)} %constant.6.clone.refs_0_, bf16[256,256]{1,0:T(8,128)(2,1)} %constant.7.clone.refs_1_, bf16[512,512]{1,0:T(8,128)(2,1)} %constant.8.clone.refs_2_), custom_call_target="tpu_custom_call" | custom-call | flops 5000000000 | bytes 10000000 | tf_op jit(solution)/shard_map/fourier/pallas_call | solution.py:162
  6.1 38.0 %all_to_all.20.r_ref = bf16[32,88,384]{2,1,0:T(8,128)(2,1)S(1)} all-to-all(bf16[32,88,384]{2,1,0:T(8,128)(2,1)S(1)} %bitcast.8), channel_id=1, replica_groups=mesh['lat'=32,'lev'=8] {'lat'}, dimensions={0} | all-to-all | bytes 4325376 | tf_op jit(solution)/shard_map/all_to_all | solution.py:358
  44.0 1.9 %legendre.1 = bf16[3584,128]{1,0:T(8,128)(2,1)S(1)} custom-call(bf16[32,88,384]{2,1,0:T(8,128)(2,1)S(1)} %all_to_all.20.r_ref), custom_call_target="tpu_custom_call" | custom-call | flops 2000000000 | bytes 4000000 | tf_op jit(solution)/shard_map/legendre/pallas_call | solution.py:256
  45.9 38.4 %all_to_all.21 = bf16[256,7,2,128]{3,2,1,0:T(2,128)(2,1)S(1)} all-to-all(bf16[256,7,2,128]{3,2,1,0:T(2,128)(2,1)S(1)} %bitcast.9), channel_id=1, replica_groups=mesh['lat'=32,'lev'=8] {'lev','lat'}, dimensions={0} | all-to-all | bytes 1835008 | tf_op jit(solution)/shard_map/all_to_all | solution.py:358
  84.3 0.0 copy-start
  84.3 1.0 covariance.1
  85.3 11.1 %all_to_all.22.g_ref = bf16[8,32,128]{2,1,0:T(8,128)(2,1)S(1)} all-to-all(bf16[8,32,128]{2,1,0:T(8,128)(2,1)S(1)} %covariance.1), channel_id=1, replica_groups=mesh['lat'=32,'lev'=8] {'lev'}, dimensions={0} | all-to-all | bytes 131072 | tf_op jit(solution)/shard_map/all_to_all | solution.py:358
  96.4 0.0 copy-done
  96.4 0.6 route.1
  97.0 12.5 %all_to_all.23.r_ref = bf16[32,16,128]{2,1,0:T(8,128)(2,1)S(1)} all-to-all(bf16[32,16,128]{2,1,0:T(8,128)(2,1)S(1)} %route.1), channel_id=1, replica_groups=mesh['lat'=32,'lev'=8] {'lat'}, dimensions={0} | all-to-all | bytes 262144 | tf_op jit(solution)/shard_map/all_to_all | solution.py:358
  109.6 1.3 %collect.1 = f32[16,16,128]{2,1,0:T(8,128)} custom-call(s32[32]{0:T(128)S(1)} %copy-done, bf16[32,16,128]{2,1,0:T(8,128)(2,1)S(1)} %all_to_all.23.r_ref), custom_call_target="tpu_custom_call" | custom-call | tf_op jit(solution)/shard_map/collect/pallas_call | solution.py:347
Async XLA Ops:
  84.3 12.1 %copy-start = (s32[32]{0:T(128)S(1)}, s32[32]{0:T(128)}, u32[]{:S(2)}) copy-start(s32[32]{0:T(128)} %counts_ref.3) | copy-start | bytes 388
